TPU v7x, 128 devices: a whole 4x4x4 slice. The times are simulated.
128 devices in a mesh: seq: 32 (over z, x, core), group: 4 (over y).
Axes of the slice: x: 4, y: 4, z: 4, core: 2. Of those that a mesh axis runs over, the one named last changes fastest.
Arguments:
- new_queries: bfloat16 [32, 8, 8, 128], P('seq', 'group'), may hold values from -6 to 6
- stored_keys: bfloat16 [32, 8, 16384, 128], P(None, 'group', 'seq'), may hold values from -6 to 6
- stored_values: bfloat16 [32, 8, 16384, 128], P(None, 'group', 'seq'), may hold values from -6 to 6
- used_length: int32 [32], replicated, may hold values from 8192 to 16384
- out_weight: bfloat16 [8, 8, 128, 5120], P('group'), may hold values from -0.0625 to 0.0625
Outputs:
- token_out: bfloat16 [32, 5120], P('seq', 'group')
All inputs are finite; a program needn't handle non-finite values.
Results may differ from a plain program's by a relative error of at most 0.0025.
Values may be sent and summed in bfloat16 or wider, within the bound.
A program may use at most 128 MiB of HBM per device.

v0:
```python
import jax
import jax.numpy as jnp
from jax import lax
from jax.sharding import PartitionSpec as P

HEAD_SIZE = 128


def per_device(new_queries, stored_keys, stored_values, used_length, out_weight):
    all_queries = lax.all_gather(new_queries, "seq", axis=0, tiled=True)
    logit = jnp.einsum(
        "bkgd,bktd->bkgt", all_queries, stored_keys, preferred_element_type=jnp.float32
    ) * HEAD_SIZE ** (-0.5)
    positions = lax.axis_index("seq") * stored_keys.shape[2] + jnp.arange(stored_keys.shape[2])
    filled = positions[None, :] < used_length[:, None]
    logit = jnp.where(filled[:, None, None, :], logit, -1e30)
    top = jnp.max(logit, axis=-1)
    part = jnp.where(filled[:, None, None, :], jnp.exp(logit - top[..., None]), 0.0)
    weight_sum = jnp.sum(part, axis=-1)
    read_sum = jnp.einsum(
        "bkgt,bktd->bkgd", part, stored_values.astype(jnp.float32), precision=lax.Precision.HIGHEST
    )
    tops, sums, parts = (
        lax.all_to_all(top[None], "seq", split_axis=1, concat_axis=0, tiled=True),
        lax.all_to_all(weight_sum[None], "seq", split_axis=1, concat_axis=0, tiled=True),
        lax.all_to_all(read_sum[None], "seq", split_axis=1, concat_axis=0, tiled=True),
    )
    best = jnp.max(tops, axis=0)
    scale = jnp.exp(tops - best)
    weight_own = jnp.sum(sums * scale, axis=0)
    read_own = jnp.sum(parts * scale[..., None], axis=0)
    read = (read_own / weight_own[..., None]).astype(jnp.bfloat16)
    term = jnp.einsum("bkgd,kgdm->bm", read, out_weight, preferred_element_type=jnp.float32)
    token_out = lax.psum_scatter(term, "group", scatter_dimension=1, tiled=True).astype(
        jnp.bfloat16
    )
    return token_out


def solution(mesh):
    in_specs = (
        P("seq", "group", None, None),
        P(None, "group", "seq", None),
        P(None, "group", "seq", None),
        P(),
        P("group", None, None, None),
    )
    out_specs = P("seq", "group")
    return jax.shard_map(
        per_device, mesh=mesh, in_specs=in_specs, out_specs=out_specs, check_vma=False
    )
```

profile of v0, /device:TPU:1, one launch (start us, length us, event | category | flops | bytes accessed | tf_op | source)
XLA Modules:
  0.0 133.9 jit_solution(4825849419178507323)
XLA Ops:
  6.5 27.1 %all_gather.3 = bf16[32,2,8,128]{3,2,1,0:T(8,128)(2,1)S(1)} all-gather(bf16[1,2,8,128]{3,2,1,0:T(8,128)(2,1)} %param.5), channel_id=1, replica_groups=mesh['seq'=32,'group'=4] {'seq'}, dimensions={0}, use_global_device_ids=true | all-gather | bytes 135168 | tf_op jit(solution)/shard_map/all_gather | solution.py:10
  33.7 0.7 broadcast_compare_fusion
  34.4 6.4 %fusion.18 = (f32[32,2,8]{2,1,0:T(2,128)}, f32[32,2,8,512]{3,2,1,0:T(8,128)S(1)}) fusion(bf16[32,2,8,128]{3,2,1,0:T(8,128)(2,1)S(1)} %all_gather.3, bf16[32,2,512,128]{3,2,1,0:T(8,128)(2,1)} %param.6, pred[32,512]{1,0:T(8,128)(4,1)S(1)} %broadcast_compare_fusion), kind=kOutput, calls=%fused_computation.25 | convolution fusion | flops 67894784 | bytes 9586688 | tf_op jit(solution)/shard_map/bkgd,bktd->bkgt/dot_general | solution.py:11
  40.8 5.1 %all-to-all-start.1 = ((f32[1,32,2,8]{3,2,0,1:T(2,128)}), f32[1,32,2,8]{3,2,0,1:T(2,128)S(1)}, u32[]{:S(2)}, u32[]{:S(2)}) async-start(f32[1,32,2,8]{3,2,0,1:T(2,128)} %bitcast.3), calls=%async_computation.1 | async-start | bytes 65536 | tf_op jit(solution)/shard_map/all_to_all | solution.py:24
  45.9 1.7 %fusion.6 = f32[32,2,8]{2,1,0:T(2,128)} fusion(f32[32,2,8,512]{3,2,1,0:T(8,128)S(1)} %get-tuple-element.6, f32[32,2,8]{2,1,0:T(2,128)} %get-tuple-element.5, pred[32,512]{1,0:T(8,128)(4,1)S(1)} %broadcast_compare_fusion), kind=kLoop, calls=%fused_computation.7 | loop fusion | flops 785920 | bytes 1069056 | tf_op jit(solution)/shard_map/reduce_sum | solution.py:19
  47.6 5.5 %all-to-all-done.1 = f32[1,32,2,8]{3,2,0,1:T(2,128)S(1)} async-done(((f32[1,32,2,8]{3,2,0,1:T(2,128)}), f32[1,32,2,8]{3,2,0,1:T(2,128)S(1)}, u32[]{:S(2)}, u32[]{:S(2)}) %all-to-all-start.1) | async-done | bytes 2080 | tf_op jit(solution)/shard_map/all_to_all | solution.py:24
  53.2 3.9 %all-to-all-start.2 = ((f32[1,32,2,8]{3,2,0,1:T(2,128)}), f32[1,32,2,8]{3,2,0,1:T(2,128)S(1)}, u32[]{:S(2)}, u32[]{:S(2)}) async-start(f32[1,32,2,8]{3,2,0,1:T(2,128)} %bitcast.5), calls=%async_computation.2 | async-start | bytes 65536 | tf_op jit(solution)/shard_map/all_to_all | solution.py:25
  57.1 6.5 %convolution_bitcast_fusion = f32[1,32,2,8,128]{4,3,2,0,1:T(8,128)} fusion(bf16[32,2,512,128]{3,2,1,0:T(8,128)(2,1)} %param.7, f32[32,2,8,512]{3,2,1,0:T(8,128)S(1)} %get-tuple-element.6, f32[32,2,8]{2,1,0:T(2,128)} %get-tuple-element.5, pred[32,512]{1,0:T(8,128)(4,1)S(1)} %broadcast_compare_fusion), kind=kOutput, calls=%fused_computation.5 | convolution fusion | flops 403177472 | bytes 9717760 | tf_op jit(solution)/shard_map/bkgt,bktd->bkgd/dot_general | solution.py:20
  63.6 0.8 all-to-all-done.2
  64.5 6.7 %all-to-all-start = ((f32[1,32,2,8,128]{4,3,2,0,1:T(8,128)}), f32[1,32,2,8,128]{4,3,2,0,1:T(8,128)S(1)}, u32[]{:S(2)}, u32[]{:S(2)}) async-start(f32[1,32,2,8,128]{4,3,2,0,1:T(8,128)} %convolution_bitcast_fusion), calls=%async_computation | async-start | bytes 524288 | tf_op jit(solution)/shard_map/all_to_all | solution.py:26
  71.1 0.0 reduce-scatter.4.cloned.1.call-start
  71.2 0.1 fusion.14
  71.3 8.7 %all-to-all-done = f32[1,32,2,8,128]{4,3,2,0,1:T(8,128)S(1)} async-done(((f32[1,32,2,8,128]{4,3,2,0,1:T(8,128)}), f32[1,32,2,8,128]{4,3,2,0,1:T(8,128)S(1)}, u32[]{:S(2)}, u32[]{:S(2)}) %all-to-all-start) | async-done | bytes 262176 | tf_op jit(solution)/shard_map/all_to_all | solution.py:26
  80.0 0.1 fusion.10
  80.1 0.1 fusion.16
  80.2 13.4 %fusion.2 = f32[5120,1]{1,0:T(8,128)} fusion(bf16[2,8,128,5120]{3,2,1,0:T(8,128)(2,1)} %param.9, bf16[2,8,128,1]{2,1,0,3:T(8,128)(2,1)S(1)} %fusion.16), kind=kOutput, calls=%fused_computation.2 | convolution fusion | flops 20971520 | bytes 20996096 | tf_op jit(solution)/shard_map/bkgd,kgdm->bm/dot_general | solution.py:33
  93.7 0.0 reduce-scatter.4.cloned.1.call-update
  93.7 31.4 %reduce-scatter.4.cloned.1.call-done = f32[1280,1]{1,0:T(8,128)} async-done(((f32[5120,1]{1,0:T(8,128)}), f32[1280,1]{1,0:T(8,128)}) %reduce-scatter.4.cloned.1.call-update) | async-done | bytes 5136
  125.1 1.9 %copy.11 = bf16[1,1280]{1,0:T(2,128)(2,1)} copy(f32[1,1280]{0,1:T(8,128)} %bitcast.41) | data formatting | bytes 7680
  (3 shorter events, 0.1 us)
Async XLA Ops:
  40.8 12.4 %all-to-all-start.1 = ((f32[1,32,2,8]{3,2,0,1:T(2,128)}), f32[1,32,2,8]{3,2,0,1:T(2,128)S(1)}, u32[]{:S(2)}, u32[]{:S(2)}) async-start(f32[1,32,2,8]{3,2,0,1:T(2,128)} %bitcast.3), calls=%async_computation.1 | async-start | bytes 65536 | tf_op jit(solution)/shard_map/all_to_all | solution.py:24
  53.2 11.3 %all-to-all-start.2 = ((f32[1,32,2,8]{3,2,0,1:T(2,128)}), f32[1,32,2,8]{3,2,0,1:T(2,128)S(1)}, u32[]{:S(2)}, u32[]{:S(2)}) async-start(f32[1,32,2,8]{3,2,0,1:T(2,128)} %bitcast.5), calls=%async_computation.2 | async-start | bytes 65536 | tf_op jit(solution)/shard_map/all_to_all | solution.py:25
  64.5 15.5 %all-to-all-start = ((f32[1,32,2,8,128]{4,3,2,0,1:T(8,128)}), f32[1,32,2,8,128]{4,3,2,0,1:T(8,128)S(1)}, u32[]{:S(2)}, u32[]{:S(2)}) async-start(f32[1,32,2,8,128]{4,3,2,0,1:T(8,128)} %convolution_bitcast_fusion), calls=%async_computation | async-start | bytes 524288 | tf_op jit(solution)/shard_map/all_to_all | solution.py:26
  71.1 54.0 %reduce-scatter.4.cloned.1.call-start = ((), (), s32[]{:S(2)}) async-start(), calls=%async_computation.4 | async-start | bytes 3276800
Sparse Core Ops, SparseCore 0:
  93.8 31.2 reduce-scatter.3
where the time goes:
time: 134 us
  waiting for transfers between devices  46.6 us (35%)
  blocking collectives  27.1 us (20%)
  matrix products  26.3 us (20%)
  starting transfers between devices  15.7 us (12%)
  between operations  13.4 us (10%)
  other arithmetic  2.8 us (2%)
  local copies, waits for them, and re-layouts  1.91 us (1%)
    unnamed x2, waiting for transfers between devices  31.5 us
    all_gather x1, blocking collectives, per_device(): all_queries = lax.all_gather(new_queries, 'seq', axis=0, tiled=True)  27.1 us
    dot_general x1, matrix products, per_device(): jnp.einsum('bkgd,kgdm->bm', read, out_weight, preferred_element_type=jnp....  13.4 us
    all_to_all x1, waiting for transfers between devices, per_device(): lax.all_to_all(read_sum[None], 'seq', split_axis=1, concat_axis=0, tiled=...  8.74 us
    all_to_all x1, starting transfers between devices, per_device(): lax.all_to_all(read_sum[None], 'seq', split_axis=1, concat_axis=0, tiled=...  6.66 us
    dot_general x1, matrix products, per_device(): jnp.einsum('bkgt,bktd->bkgd', part, stored_values.astype(jnp.float32), pr...  6.5 us
    dot_general x1, matrix products, per_device(): jnp.einsum('bkgd,bktd->bkgt', all_queries, stored_keys, preferred_element...  6.36 us
    all_to_all x1, waiting for transfers between devices, per_device(): lax.all_to_all(top[None], 'seq', split_axis=1, concat_axis=0, tiled=True)  5.54 us
  transfers between devices with their start and end apart: 4, of which 4 were waited for; matrix products, arithmetic and copies ran while one was open for 6% of the time, Pallas kernels for 0%

commit v1 on v0

v1 whole, which is shorter than its diff:
```python
import functools

import jax
import jax.numpy as jnp
from jax import lax
from jax.experimental import pallas as pl
from jax.experimental.pallas import tpu as pltpu
from jax.sharding import PartitionSpec as P

MESH = pl.DeviceIdType.MESH
SEQ, GRP = 32, 4
HEADS, GROUP, HEAD = 2, 8, 128
ROWS = HEADS * GROUP
STRETCH = 512
COLS = 1280
UNIT = 4
STEPS = SEQ // UNIT
TO_EXP2 = HEAD ** (-0.5) * 1.4426950408889634


def near_first(i):
    return i + (i // 2) * (5 - 2 * i)


def offset_of(me, dz, dx, dc):
    z, x, c = me // 8, (me // 2) % 4, me % 2
    return ((z + dz) % 4) * 8 + ((x + dx) % 4) * 2 + (c + dc) % 2


def sequence_of(me, step, u):
    dz = near_first(step // 2)
    dx = near_first(2 * (step % 2) + u // 2)
    return offset_of(me, dz, dx, u % 2)


def kernel(
    q_hbm, k_hbm, v_hbm, len_hbm, w_hbm, out_ref,
    kbuf, vbuf, wbuf, qbuf, lens, logits, psend, ssend, parts, stats, rows, ysend, ybuf,
    local_sem, k_sem, v_sem, w_sem, q_send, q_recv, p_send, p_recv, s_send, s_recv, y_send, y_recv,
):
    me = lax.axis_index("seq")
    grp = lax.axis_index("group")

    barrier = pltpu.get_barrier_semaphore()
    for i in range(1, SEQ):
        pl.semaphore_signal(barrier, 1, device_id={"seq": (me + i) % SEQ}, device_id_type=MESH)
    for i in range(1, GRP):
        pl.semaphore_signal(barrier, 1, device_id={"group": (grp + i) % GRP}, device_id_type=MESH)

    q_copy = pltpu.make_async_copy(q_hbm.at[0], qbuf.at[me], local_sem.at[0])
    len_copy = pltpu.make_async_copy(len_hbm, lens, local_sem.at[1])
    q_copy.start()
    len_copy.start()

    def k_copy(step, u):
        j = step * UNIT + u
        return pltpu.make_async_copy(k_hbm.at[sequence_of(me, step, u)], kbuf.at[j], k_sem.at[j])

    def v_copy(step, u):
        j = step * UNIT + u
        return pltpu.make_async_copy(v_hbm.at[sequence_of(me, step, u)], vbuf.at[j], v_sem.at[j])

    @pl.loop(0, STEPS)
    def _(step):
        for u in range(UNIT):
            k_copy(step, u).start()
        for u in range(UNIT):
            v_copy(step, u).start()

    def owner_of(quarter):
        return (grp + (2, 1, 3, 0)[quarter]) % GRP

    def w_copy(quarter):
        first = pl.multiple_of(owner_of(quarter) * COLS, 128)
        return pltpu.make_async_copy(
            w_hbm.at[:, :, :, pl.ds(first, COLS)], wbuf.at[quarter], w_sem.at[quarter]
        )

    for quarter in range(GRP):
        w_copy(quarter).start()

    def q_remote(source, i, peer):
        return pltpu.make_async_remote_copy(
            src_ref=qbuf.at[source], dst_ref=qbuf.at[source],
            send_sem=q_send.at[i], recv_sem=q_recv.at[source],
            device_id={"seq": peer}, device_id_type=MESH,
        )

    def peer_at(i):
        return sequence_of(me, i // UNIT, i % UNIT)

    q_copy.wait()
    len_copy.wait()
    pl.semaphore_wait(barrier, SEQ - 1 + GRP - 1)
    for i in range(SEQ - 1, 0, -1):
        q_remote(me, i, peer_at(i)).start()

    def scores(step, slot):
        for u in range(UNIT):
            b = sequence_of(me, step, u)
            if u == 0:

                @pl.when(step > 0)
                def _():
                    q_remote(b, 0, b).wait_recv()
            else:
                q_remote(b, 0, b).wait_recv()
            k_copy(step, u).wait()
        lane = lax.broadcasted_iota(jnp.int32, (ROWS, STRETCH), 1) + me * STRETCH
        for u in range(UNIT):
            j = step * UNIT + u
            b = sequence_of(me, step, u)
            zero = jnp.zeros((GROUP, HEAD), jnp.float32)
            q0 = qbuf[b, 0].astype(jnp.float32)
            q1 = qbuf[b, 1].astype(jnp.float32)
            q = jnp.concatenate(
                [jnp.concatenate([q0, zero], axis=1), jnp.concatenate([zero, q1], axis=1)], axis=0
            ).astype(jnp.bfloat16)
            k = jnp.concatenate([kbuf[j, 0], kbuf[j, 1]], axis=1)
            logit = lax.dot_general(
                q, k, (((1,), (1,)), ((), ())), preferred_element_type=jnp.float32
            )
            logits[slot, u] = jnp.where(lane < lens[b], logit, -1e30)

    def reads(step, slot):
        row = lax.broadcasted_iota(jnp.int32, (ROWS, HEAD), 0)
        lane = lax.broadcasted_iota(jnp.int32, (ROWS, HEAD), 1)
        for u in range(UNIT):
            v_copy(step, u).wait()
        for u in range(UNIT):
            j = step * UNIT + u
            logit = logits[slot, u]
            top = jnp.max(logit, axis=1, keepdims=True)
            part = jnp.exp2((logit - top) * TO_EXP2)
            total = jnp.sum(part, axis=1, keepdims=True)
            high = part.astype(jnp.bfloat16)
            low = (part - high.astype(jnp.float32)).astype(jnp.bfloat16)
            v = jnp.concatenate([vbuf[j, 0], vbuf[j, 1]], axis=1)
            both = jnp.dot(
                jnp.concatenate([high, low], axis=0), v, preferred_element_type=jnp.float32
            )
            both = both[:ROWS] + both[ROWS:]
            psend[j] = jnp.concatenate([both[:GROUP, :HEAD], both[GROUP:, HEAD:]], axis=0)
            pair = jnp.where(lane == row, top, jnp.where(lane == row + ROWS, total, 0.0))
            ssend[j] = jnp.sum(pair, axis=0, keepdims=True)

    def p_remote(source, j, peer):
        return pltpu.make_async_remote_copy(
            src_ref=psend.at[j], dst_ref=parts.at[source],
            send_sem=p_send.at[j], recv_sem=p_recv.at[source],
            device_id={"seq": peer}, device_id_type=MESH,
        )

    def s_remote(source, j, peer):
        return pltpu.make_async_remote_copy(
            src_ref=ssend.at[j], dst_ref=stats.at[source],
            send_sem=s_send.at[j], recv_sem=s_recv.at[source],
            device_id={"seq": peer}, device_id_type=MESH,
        )

    def send(step):
        for u in range(UNIT):
            j = step * UNIT + u

            def go():
                s_remote(me, j, sequence_of(me, step, u)).start()
                p_remote(me, j, sequence_of(me, step, u)).start()

            if u == 0:
                pl.when(step > 0)(go)
            else:
                go()

    scores(0, 0)

    @pl.loop(0, STEPS - 1)
    def _(step):
        scores(step + 1, (step + 1) % 2)
        reads(step, step % 2)
        send(step)

    reads(STEPS - 1, (STEPS - 1) % 2)
    send(STEPS - 1)
    parts[me] = psend[0]
    stats[me] = ssend[0]

    for i in range(1, SEQ):
        s_remote(peer_at(i), 0, me).wait_recv()
    stat = stats[:, 0, :]
    best = jnp.max(stat, axis=0, keepdims=True)
    scale = jnp.exp2((stat - best) * TO_EXP2)
    sums = pltpu.roll(stat, HEAD - ROWS, axis=1)
    weight = scale / jnp.sum(sums * scale, axis=0, keepdims=True)
    weight = weight.T[:ROWS]

    for i in range(1, SEQ):
        p_remote(peer_at(i), 0, me).wait_recv()
    read = jnp.zeros((ROWS, HEAD), jnp.float32)
    for i in range(SEQ):
        read = read + parts[i] * weight[:, i : i + 1]
    rows[...] = read.astype(jnp.bfloat16).astype(jnp.float32)
    spread = jnp.concatenate(
        [jnp.broadcast_to(rows[r : r + 1, :], (GROUP, HEAD)) for r in range(ROWS)], axis=1
    ).astype(jnp.bfloat16)

    def y_remote(source, quarter, peer):
        return pltpu.make_async_remote_copy(
            src_ref=ysend.at[quarter], dst_ref=ybuf.at[source],
            send_sem=y_send.at[quarter], recv_sem=y_recv.at[source],
            device_id={"group": peer}, device_id_type=MESH,
        )

    for quarter in range(GRP):
        w_copy(quarter).wait()
        term = jnp.dot(
            spread,
            wbuf[quarter].reshape(ROWS * HEAD, COLS),
            preferred_element_type=jnp.float32,
        )
        for n in range(COLS // 128):
            ysend[quarter, n : n + 1, :] = term[0:1, n * 128 : (n + 1) * 128]
        if quarter < GRP - 1:
            y_remote(grp, quarter, owner_of(quarter)).start()

    for i in range(1, GRP):
        y_remote((grp + i) % GRP, 0, grp).wait_recv()
    token = ysend[GRP - 1]
    for i in range(1, GRP):
        token = token + ybuf[(grp + i) % GRP]
    for n in range(COLS // 128):
        out_ref[0:1, n * 128 : (n + 1) * 128] = token[n : n + 1, :].astype(out_ref.dtype)

    for i in range(1, SEQ):
        q_remote(me, i, peer_at(i)).wait_send()
        p_remote(me, i, peer_at(i)).wait_send()
        s_remote(me, i, peer_at(i)).wait_send()
    for quarter in range(GRP - 1):
        y_remote(grp, quarter, owner_of(quarter)).wait_send()


def per_device(new_queries, stored_keys, stored_values, used_length, out_weight):
    hbm = pl.BlockSpec(memory_space=pl.ANY)
    dma = pltpu.SemaphoreType.DMA
    return pl.pallas_call(
        kernel,
        out_shape=jax.ShapeDtypeStruct((1, COLS), jnp.bfloat16),
        in_specs=[hbm] * 5,
        out_specs=pl.BlockSpec(memory_space=pltpu.VMEM),
        scratch_shapes=[
            pltpu.VMEM((SEQ, HEADS, STRETCH, HEAD), jnp.bfloat16),
            pltpu.VMEM((SEQ, HEADS, STRETCH, HEAD), jnp.bfloat16),
            pltpu.VMEM((GRP, HEADS, GROUP, HEAD, COLS), jnp.bfloat16),
            pltpu.VMEM((SEQ, HEADS, GROUP, HEAD), jnp.bfloat16),
            pltpu.SMEM((SEQ,), jnp.int32),
            pltpu.VMEM((2, UNIT, ROWS, STRETCH), jnp.float32),
            pltpu.VMEM((SEQ, ROWS, HEAD), jnp.float32),
            pltpu.VMEM((SEQ, 1, 128), jnp.float32),
            pltpu.VMEM((SEQ, ROWS, HEAD), jnp.float32),
            pltpu.VMEM((SEQ, 1, 128), jnp.float32),
            pltpu.VMEM((ROWS, HEAD), jnp.float32),
            pltpu.VMEM((GRP, COLS // 128, 128), jnp.float32),
            pltpu.VMEM((GRP, COLS // 128, 128), jnp.float32),
            dma((2,)), dma((SEQ,)), dma((SEQ,)), dma((GRP,)),
            dma((SEQ,)), dma((SEQ,)), dma((SEQ,)), dma((SEQ,)), dma((SEQ,)), dma((SEQ,)),
            dma((GRP,)), dma((GRP,)),
        ],
        compiler_params=pltpu.CompilerParams(
            collective_id=0, has_side_effects=True, vmem_limit_bytes=60 * 1024 * 1024
        ),
        name="decode",
    )(new_queries, stored_keys, stored_values, used_length, out_weight)


def solution(mesh):
    in_specs = (
        P("seq", "group", None, None),
        P(None, "group", "seq", None),
        P(None, "group", "seq", None),
        P(),
        P("group", None, None, None),
    )
    return jax.shard_map(
        per_device, mesh=mesh, in_specs=in_specs, out_specs=P("seq", "group"), check_vma=False
    )
```

time: 134 us -> 32.4 us (0.24)
  waiting for transfers between devices: 46.6 us -> 0 us
  Pallas kernels: 0 us -> 31 us
  blocking collectives: 27.1 us -> 0 us
  matrix products: 26.3 us -> 0 us
  starting transfers between devices: 15.7 us -> 0 us
  between operations: 13.4 us -> 0.01 us
  other arithmetic: 2.8 us -> 0 us
    unnamed x2 -> x0, waiting for transfers between devices: 31.5 us -> none
    pallas_call x0 -> x1, Pallas kernels: none -> 31 us  [per_device(): pl.pallas_call(kernel, out_shape=jax.ShapeDtypeStruct((1, COLS), jnp.bflo...]
    all_gather x1 -> x0, blocking collectives: 27.1 us -> none  [per_device(): all_queries = lax.all_gather(new_queries, 'seq', axis=0, tiled=True)]
    dot_general x3 -> x0, matrix products: 26.3 us -> none  [the longest x1 13.4 us: per_device(): jnp.einsum('bkgd,kgdm->bm', read, out_weight, preferred_element_type=jnp....]
    all_to_all x3 -> x0, starting transfers between devices: 15.7 us -> none  [the longest x1 6.66 us: per_device(): lax.all_to_all(read_sum[None], 'seq', split_axis=1, concat_axis=0, tiled=...]
    all_to_all x3 -> x0, waiting for transfers between devices: 15.1 us -> none  [the longest x1 8.74 us: per_device(): lax.all_to_all(read_sum[None], 'seq', split_axis=1, concat_axis=0, tiled=...]
    reduce_sum x3 -> x0, other arithmetic: 1.92 us -> none  [the longest x1 1.74 us: per_device(): weight_sum = jnp.sum(part, axis=-1)]
  transfers between devices with their start and end apart: 4 -> 0, of which waited for: 4 -> 0; matrix products, arithmetic and copies ran while one was open for 6% -> 0% of each run, Pallas kernels for 0% -> 0%
where the time goes in v1:
time: 32.4 us; the launch traced here: 32.3 us
  Pallas kernels  31 us (96%)
  local copies, waits for them, and re-layouts  1.29 us (4%)
    pallas_call x1, Pallas kernels, per_device(): pl.pallas_call(kernel, out_shape=jax.ShapeDtypeStruct((1, COLS), jnp.bflo...  31 us
    unnamed x1, local copies, waits for them, and re-layouts  1.29 us

profile of v1, /device:TPU:1, one launch (start us, length us, event | category | flops | bytes accessed | tf_op | source)
XLA Modules:
  0.0 32.3 jit_solution(2938415253467002272)
XLA Ops:
  0.0 31.0 %decode.1 = bf16[1,1280]{1,0:T(2,128)(2,1)} custom-call(bf16[1,2,8,128]{3,2,1,0:T(8,128)(2,1)} %q_hbm.1, bf16[32,2,512,128]{3,2,1,0:T(8,128)(2,1)} %k_hbm.1, bf16[32,2,512,128]{3,2,1,0:T(8,128)(2,1)} %v_hbm.1, s32[32]{0:T(128)} %len_hbm.1, bf16[2,8,128,5120]{3,2,1,0:T(8,128)(2,1)} %w_hbm.1), custom_call_target="tpu_custom_call" | custom-call | tf_op jit(solution)/shard_map/decode/pallas_call | solution.py:244
  31.0 1.3 %copy.7 = bf16[1,1280]{1,0:T(2,128)(2,1)} copy(bf16[1,1280]{1,0:T(2,128)(2,1)} %decode.1) | data formatting | bytes 5120

commit v2 on v1

v2 whole, which is shorter than its diff:
```python
import jax
import jax.numpy as jnp
from jax import lax
from jax.experimental import pallas as pl
from jax.experimental.pallas import tpu as pltpu
from jax.sharding import PartitionSpec as P

MESH = pl.DeviceIdType.MESH
SEQ, GRP = 32, 4
LAYERS, ROW = 4, 8
HEADS, GROUP, HEAD = 2, 8, 128
ROWS = HEADS * GROUP
STRETCH = 512
COLS = 1280
UNIT = 4
STEPS = SEQ // UNIT
TO_EXP2 = HEAD ** (-0.5) * 1.4426950408889634


def kernel(
    q_hbm, k_hbm, v_hbm, len_hbm, w_hbm, out_ref,
    kbuf, vbuf, wbuf, qbuf, lens, logits, psend, ssend, parts, stats, rows, ysend, ybuf,
    local_sem, k_sem, v_sem, w_sem, q_send, q_recv, p_send, p_recv, s_send, s_recv, y_send, y_recv,
):
    me = lax.axis_index("seq")
    grp = lax.axis_index("group")
    layer, place = lax.div(me, ROW), lax.rem(me, ROW)
    first = layer * ROW

    def mate(i):
        return first + lax.rem(place + i, ROW)

    def column(i):
        return lax.rem(layer + i, LAYERS) * ROW + place

    def across(i):
        return lax.rem(grp + i, GRP)

    barrier = pltpu.get_barrier_semaphore()
    for i in range(1, LAYERS):
        pl.semaphore_signal(barrier, 1, device_id={"seq": column(i)}, device_id_type=MESH)
    for i in range(1, ROW):
        pl.semaphore_signal(barrier, 1, device_id={"seq": mate(i)}, device_id_type=MESH)
    for i in range(1, GRP):
        pl.semaphore_signal(barrier, 1, device_id={"group": across(i)}, device_id_type=MESH)

    q_copy = pltpu.make_async_copy(q_hbm.at[0], qbuf.at[me], local_sem.at[0])
    len_copy = pltpu.make_async_copy(len_hbm, lens, local_sem.at[1])
    q_copy.start()
    len_copy.start()

    def k_copy(step):
        some = pl.ds(step * UNIT, UNIT)
        return pltpu.make_async_copy(k_hbm.at[some], kbuf.at[some], k_sem.at[step])

    def v_copy(step):
        some = pl.ds(step * UNIT, UNIT)
        return pltpu.make_async_copy(v_hbm.at[some], vbuf.at[some], v_sem.at[step])

    def owner_of(quarter):
        return across((2, 1, 3, 0)[quarter])

    def w_copy(quarter):
        start = pl.multiple_of(owner_of(quarter) * COLS, 128)
        return pltpu.make_async_copy(
            w_hbm.at[:, :, :, pl.ds(start, COLS)], wbuf.at[quarter], w_sem.at[quarter]
        )

    for step in range(STEPS):
        k_copy(step).start()
        v_copy(step).start()
    for quarter in range(GRP):
        w_copy(quarter).start()

    def q_remote(source, peer):
        return pltpu.make_async_remote_copy(
            src_ref=qbuf.at[source], dst_ref=qbuf.at[source],
            send_sem=q_send, recv_sem=q_recv.at[source],
            device_id={"seq": peer}, device_id_type=MESH,
        )

    q_copy.wait()
    len_copy.wait()
    pl.semaphore_wait(barrier, LAYERS - 1 + ROW - 1 + GRP - 1)
    for i in range(1, ROW):
        q_remote(me, mate(i)).start()
    for i in range(1, LAYERS):
        q_remote(me, column(i)).start()

    @pl.loop(0, ROW)
    def _(i):
        source = first + i

        @pl.when(i != place)
        def _():
            q_remote(source, me).wait_recv()
            for other in range(1, LAYERS):
                q_remote(source, column(other)).start()

    def scores(step, slot):
        @pl.when(lax.div(step, ROW // UNIT) != layer)
        def _():
            for u in range(UNIT):
                q_remote(step * UNIT + u, me).wait_recv()

        k_copy(step).wait()
        lane = lax.broadcasted_iota(jnp.int32, (ROWS, STRETCH), 1) + me * STRETCH
        for u in range(UNIT):
            b = step * UNIT + u
            zero = jnp.zeros((GROUP, HEAD), jnp.float32)
            q0 = qbuf[b, 0].astype(jnp.float32)
            q1 = qbuf[b, 1].astype(jnp.float32)
            q = jnp.concatenate(
                [jnp.concatenate([q0, zero], axis=1), jnp.concatenate([zero, q1], axis=1)], axis=0
            ).astype(jnp.bfloat16)
            k = jnp.concatenate([kbuf[b, 0], kbuf[b, 1]], axis=1)
            logit = lax.dot_general(
                q, k, (((1,), (1,)), ((), ())), preferred_element_type=jnp.float32
            )
            logits[slot, u] = jnp.where(lane < lens[b], logit, -1e30)

    def reads(step, slot):
        row = lax.broadcasted_iota(jnp.int32, (ROWS, HEAD), 0)
        lane = lax.broadcasted_iota(jnp.int32, (ROWS, HEAD), 1)
        v_copy(step).wait()
        for u in range(UNIT):
            b = step * UNIT + u
            logit = logits[slot, u]
            top = jnp.max(logit, axis=1, keepdims=True)
            part = jnp.exp2((logit - top) * TO_EXP2)
            total = jnp.sum(part, axis=1, keepdims=True)
            high = part.astype(jnp.bfloat16)
            low = (part - high.astype(jnp.float32)).astype(jnp.bfloat16)
            v = jnp.concatenate([vbuf[b, 0], vbuf[b, 1]], axis=1)
            both = jnp.dot(
                jnp.concatenate([high, low], axis=0), v, preferred_element_type=jnp.float32
            )
            both = both[:ROWS] + both[ROWS:]
            psend[b] = jnp.concatenate([both[:GROUP, :HEAD], both[GROUP:, HEAD:]], axis=0)
            pair = jnp.where(lane == row, top, jnp.where(lane == row + ROWS, total, 0.0))
            ssend[b] = jnp.sum(pair, axis=0, keepdims=True)

    def p_remote(b):
        return pltpu.make_async_remote_copy(
            src_ref=psend.at[b], dst_ref=parts.at[me], send_sem=p_send, recv_sem=p_recv,
            device_id={"seq": b}, device_id_type=MESH,
        )

    def s_remote(b):
        return pltpu.make_async_remote_copy(
            src_ref=ssend.at[b], dst_ref=stats.at[me], send_sem=s_send, recv_sem=s_recv,
            device_id={"seq": b}, device_id_type=MESH,
        )

    def send(step):
        for u in range(UNIT):
            b = step * UNIT + u

            @pl.when(b != me)
            def _():
                s_remote(b).start()
                p_remote(b).start()

    scores(0, 0)

    @pl.loop(0, STEPS - 1)
    def _(step):
        scores(step + 1, lax.rem(step + 1, 2))
        reads(step, lax.rem(step, 2))
        send(step)

    reads(STEPS - 1, (STEPS - 1) % 2)
    send(STEPS - 1)
    parts[me] = psend[me]
    stats[me] = ssend[me]
    for quarter in range(GRP):
        w_copy(quarter).wait()

    def all_but_one(ref, send_sem, recv_sem):
        most = ref.at[pl.ds(0, SEQ - 1)]
        return pltpu.make_async_remote_copy(
            src_ref=most, dst_ref=most, send_sem=send_sem, recv_sem=recv_sem,
            device_id={"seq": me}, device_id_type=MESH,
        )

    all_but_one(stats, s_send, s_recv).wait_recv()
    stat = stats[:, 0, :]
    best = jnp.max(stat, axis=0, keepdims=True)
    scale = jnp.exp2((stat - best) * TO_EXP2)
    sums = pltpu.roll(stat, HEAD - ROWS, axis=1)
    weight = scale / jnp.sum(sums * scale, axis=0, keepdims=True)
    weight = weight.T[:ROWS]

    all_but_one(parts, p_send, p_recv).wait_recv()
    read = jnp.zeros((ROWS, HEAD), jnp.float32)
    for i in range(SEQ):
        read = read + parts[i] * weight[:, i : i + 1]
    rows[...] = read.astype(jnp.bfloat16).astype(jnp.float32)
    spread = jnp.concatenate(
        [jnp.broadcast_to(rows[r : r + 1, :], (GROUP, HEAD)) for r in range(ROWS)], axis=1
    ).astype(jnp.bfloat16)

    def y_remote(source, quarter, peer):
        return pltpu.make_async_remote_copy(
            src_ref=ysend.at[quarter], dst_ref=ybuf.at[source],
            send_sem=y_send.at[quarter], recv_sem=y_recv.at[source],
            device_id={"group": peer}, device_id_type=MESH,
        )

    for quarter in range(GRP):
        term = jnp.dot(
            spread,
            wbuf[quarter].reshape(ROWS * HEAD, COLS),
            preferred_element_type=jnp.float32,
        )
        for n in range(COLS // 128):
            ysend[quarter, n : n + 1, :] = term[0:1, n * 128 : (n + 1) * 128]
        if quarter < GRP - 1:
            y_remote(grp, quarter, owner_of(quarter)).start()

    for i in range(1, GRP):
        y_remote(across(i), 0, grp).wait_recv()
    token = ysend[GRP - 1]
    for i in range(1, GRP):
        token = token + ybuf[across(i)]
    for n in range(COLS // 128):
        out_ref[0:1, n * 128 : (n + 1) * 128] = token[n : n + 1, :].astype(out_ref.dtype)

    all_but_one(qbuf, q_send, q_recv.at[0]).wait_send()
    all_but_one(parts, p_send, p_recv).wait_send()
    all_but_one(stats, s_send, s_recv).wait_send()
    for quarter in range(GRP - 1):
        y_remote(grp, quarter, owner_of(quarter)).wait_send()


def per_device(new_queries, stored_keys, stored_values, used_length, out_weight):
    hbm = pl.BlockSpec(memory_space=pl.ANY)
    dma = pltpu.SemaphoreType.DMA
    return pl.pallas_call(
        kernel,
        out_shape=pltpu.VMEM((1, COLS), jnp.bfloat16),
        in_specs=[hbm] * 5,
        out_specs=pl.BlockSpec(memory_space=pltpu.VMEM),
        scratch_shapes=[
            pltpu.VMEM((SEQ, HEADS, STRETCH, HEAD), jnp.bfloat16),
            pltpu.VMEM((SEQ, HEADS, STRETCH, HEAD), jnp.bfloat16),
            pltpu.VMEM((GRP, HEADS, GROUP, HEAD, COLS), jnp.bfloat16),
            pltpu.VMEM((SEQ, HEADS, GROUP, HEAD), jnp.bfloat16),
            pltpu.SMEM((SEQ,), jnp.int32),
            pltpu.VMEM((2, UNIT, ROWS, STRETCH), jnp.float32),
            pltpu.VMEM((SEQ, ROWS, HEAD), jnp.float32),
            pltpu.VMEM((SEQ, 1, 128), jnp.float32),
            pltpu.VMEM((SEQ, ROWS, HEAD), jnp.float32),
            pltpu.VMEM((SEQ, 1, 128), jnp.float32),
            pltpu.VMEM((ROWS, HEAD), jnp.float32),
            pltpu.VMEM((GRP, COLS // 128, 128), jnp.float32),
            pltpu.VMEM((GRP, COLS // 128, 128), jnp.float32),
            dma((2,)), dma((STEPS,)), dma((STEPS,)), dma((GRP,)),
            dma(()), dma((SEQ,)), dma(()), dma(()), dma(()), dma(()),
            dma((GRP,)), dma((GRP,)),
        ],
        compiler_params=pltpu.CompilerParams(
            collective_id=0, has_side_effects=True, vmem_limit_bytes=60 * 1024 * 1024
        ),
        name="decode",
    )(new_queries, stored_keys, stored_values, used_length, out_weight)


def solution(mesh):
    in_specs = (
        P("seq", "group", None, None),
        P(None, "group", "seq", None),
        P(None, "group", "seq", None),
        P(),
        P("group", None, None, None),
    )
    return jax.shard_map(
        per_device, mesh=mesh, in_specs=in_specs, out_specs=P("seq", "group"), check_vma=False
    )
```

time: 32.4 us -> 30.2 us (0.932)
  the two profiles are of different devices: /device:TPU:1 before, /device:TPU:96 now
where the time goes in v2:
time: 30.2 us; the launch traced here: 30.1 us
  Pallas kernels  29.5 us (98%)
  local copies, waits for them, and re-layouts  0.6 us (2%)
    pallas_call x1, Pallas kernels, per_device(): pl.pallas_call(kernel, out_shape=pltpu.VMEM((1, COLS), jnp.bfloat16), in_...  29.5 us

profile of v2, /device:TPU:96, one launch (start us, length us, event | category | flops | bytes accessed | tf_op | source)
XLA Modules:
  0.0 30.1 jit_solution(285383667826870957)
XLA Ops:
  0.0 29.5 %decode.1 = bf16[1,1280]{1,0:T(2,128)(2,1)S(1)} custom-call(bf16[1,2,8,128]{3,2,1,0:T(8,128)(2,1)} %q_hbm.1, bf16[32,2,512,128]{3,2,1,0:T(8,128)(2,1)} %k_hbm.1, bf16[32,2,512,128]{3,2,1,0:T(8,128)(2,1)} %v_hbm.1, s32[32]{0:T(128)} %len_hbm.1, bf16[2,8,128,5120]{3,2,1,0:T(8,128)(2,1)} %w_hbm.1), custom_call_target="tpu_custom_call" | custom-call | tf_op jit(solution)/shard_map/decode/pallas_call | solution.py:239
  29.5 0.6 %copy.7 = bf16[1,1280]{1,0:T(2,128)(2,1)} copy(bf16[1,1280]{1,0:T(2,128)(2,1)S(1)} %decode.1) | data formatting | bytes 5120

commit v3 on v2

--- a/solution.py
+++ b/solution.py
@@ -7,7 +7,7 @@
 
 MESH = pl.DeviceIdType.MESH
 SEQ, GRP = 32, 4
-LAYERS, ROW = 4, 8
+LAYERS, ROW, PAIR = 4, 8, 2
 HEADS, GROUP, HEAD = 2, 8, 128
 ROWS = HEADS * GROUP
 STRETCH = 512
@@ -36,13 +36,18 @@
     def across(i):
         return lax.rem(grp + i, GRP)
 
+    core = lax.rem(me, PAIR)
+    chip = me - core
+
     barrier = pltpu.get_barrier_semaphore()
     for i in range(1, LAYERS):
         pl.semaphore_signal(barrier, 1, device_id={"seq": column(i)}, device_id_type=MESH)
     for i in range(1, ROW):
         pl.semaphore_signal(barrier, 1, device_id={"seq": mate(i)}, device_id_type=MESH)
     for i in range(1, GRP):
-        pl.semaphore_signal(barrier, 1, device_id={"group": across(i)}, device_id_type=MESH)
+        for other in range(PAIR):
+            there = {"seq": chip + other, "group": across(i)}
+            pl.semaphore_signal(barrier, 1, device_id=there, device_id_type=MESH)
 
     q_copy = pltpu.make_async_copy(q_hbm.at[0], qbuf.at[me], local_sem.at[0])
     len_copy = pltpu.make_async_copy(len_hbm, lens, local_sem.at[1])
@@ -63,14 +68,14 @@
     def w_copy(quarter):
         start = pl.multiple_of(owner_of(quarter) * COLS, 128)
         return pltpu.make_async_copy(
-            w_hbm.at[:, :, :, pl.ds(start, COLS)], wbuf.at[quarter], w_sem.at[quarter]
+            w_hbm.at[core, :, :, pl.ds(start, COLS)], wbuf.at[quarter], w_sem.at[quarter]
         )
 
     for step in range(STEPS):
-        k_copy(step).start()
-        v_copy(step).start()
+        k_copy(step).start(priority=1)
+        v_copy(step).start(priority=1)
     for quarter in range(GRP):
-        w_copy(quarter).start()
+        w_copy(quarter).start(priority=1)
 
     def q_remote(source, peer):
         return pltpu.make_async_remote_copy(
@@ -81,26 +86,27 @@
 
     q_copy.wait()
     len_copy.wait()
-    pl.semaphore_wait(barrier, LAYERS - 1 + ROW - 1 + GRP - 1)
+    pl.semaphore_wait(barrier, LAYERS - 1 + ROW - 1 + PAIR * (GRP - 1))
+    for i in range(1, LAYERS):
+        q_remote(me, column(i)).start()
     for i in range(1, ROW):
         q_remote(me, mate(i)).start()
-    for i in range(1, LAYERS):
-        q_remote(me, column(i)).start()
-
-    @pl.loop(0, ROW)
+
+    @pl.loop(0, LAYERS)
     def _(i):
-        source = first + i
-
-        @pl.when(i != place)
+        source = i * ROW + place
+
+        @pl.when(i != layer)
         def _():
             q_remote(source, me).wait_recv()
-            for other in range(1, LAYERS):
-                q_remote(source, column(other)).start()
+            for other in range(1, ROW):
+                q_remote(source, mate(other)).start()
 
     def scores(step, slot):
-        @pl.when(lax.div(step, ROW // UNIT) != layer)
-        def _():
-            for u in range(UNIT):
+        for u in range(UNIT):
+
+            @pl.when(lax.rem(step * UNIT + u, ROW) != place)
+            def _():
                 q_remote(step * UNIT + u, me).wait_recv()
 
         k_copy(step).wait()
@@ -123,6 +129,7 @@
         row = lax.broadcasted_iota(jnp.int32, (ROWS, HEAD), 0)
         lane = lax.broadcasted_iota(jnp.int32, (ROWS, HEAD), 1)
         v_copy(step).wait()
+        results = []
         for u in range(UNIT):
             b = step * UNIT + u
             logit = logits[slot, u]
@@ -135,10 +142,17 @@
             both = jnp.dot(
                 jnp.concatenate([high, low], axis=0), v, preferred_element_type=jnp.float32
             )
-            both = both[:ROWS] + both[ROWS:]
-            psend[b] = jnp.concatenate([both[:GROUP, :HEAD], both[GROUP:, HEAD:]], axis=0)
-            pair = jnp.where(lane == row, top, jnp.where(lane == row + ROWS, total, 0.0))
-            ssend[b] = jnp.sum(pair, axis=0, keepdims=True)
+            results.append((both[:ROWS] + both[ROWS:], top, total))
+        for u in range(0, UNIT, PAIR):
+            for head in range(HEADS):
+                own = slice(head * GROUP, (head + 1) * GROUP)
+                here = slice(head * HEAD, (head + 1) * HEAD)
+                two = results[u : u + PAIR]
+                top = jnp.concatenate([r[1][own] for r in two], axis=0)
+                total = jnp.concatenate([r[2][own] for r in two], axis=0)
+                psend[step * UNIT + u + head] = jnp.concatenate([r[0][own, here] for r in two], axis=0)
+                pair = jnp.where(lane == row, top, jnp.where(lane == row + ROWS, total, 0.0))
+                ssend[step * UNIT + u + head] = jnp.sum(pair, axis=0, keepdims=True)
 
     def p_remote(b):
         return pltpu.make_async_remote_copy(
@@ -196,41 +210,51 @@
     for i in range(SEQ):
         read = read + parts[i] * weight[:, i : i + 1]
     rows[...] = read.astype(jnp.bfloat16).astype(jnp.float32)
+    even = lax.broadcasted_iota(jnp.int32, (GROUP, HEAD), 0) == 0
     spread = jnp.concatenate(
-        [jnp.broadcast_to(rows[r : r + 1, :], (GROUP, HEAD)) for r in range(ROWS)], axis=1
+        [jnp.where(even, rows[r : r + 1, :], rows[GROUP + r : GROUP + r + 1, :]) for r in range(GROUP)],
+        axis=1,
     ).astype(jnp.bfloat16)
 
-    def y_remote(source, quarter, peer):
-        return pltpu.make_async_remote_copy(
-            src_ref=ysend.at[quarter], dst_ref=ybuf.at[source],
-            send_sem=y_send.at[quarter], recv_sem=y_recv.at[source],
-            device_id={"group": peer}, device_id_type=MESH,
+    mine = grp * PAIR + core
+
+    def y_remote(quarter, token, peer):
+        return pltpu.make_async_remote_copy(
+            src_ref=ysend.at[quarter, token], dst_ref=ybuf.at[mine], send_sem=y_send, recv_sem=y_recv,
+            device_id={"seq": chip + token, "group": peer}, device_id_type=MESH,
         )
 
     for quarter in range(GRP):
         term = jnp.dot(
-            spread,
-            wbuf[quarter].reshape(ROWS * HEAD, COLS),
-            preferred_element_type=jnp.float32,
-        )
-        for n in range(COLS // 128):
-            ysend[quarter, n : n + 1, :] = term[0:1, n * 128 : (n + 1) * 128]
+            spread, wbuf[quarter].reshape(GROUP * HEAD, COLS), preferred_element_type=jnp.float32
+        )
+        for token in range(PAIR):
+            for n in range(COLS // 128):
+                ysend[quarter, token, n : n + 1, :] = term[token : token + 1, n * 128 : (n + 1) * 128]
         if quarter < GRP - 1:
-            y_remote(grp, quarter, owner_of(quarter)).start()
-
-    for i in range(1, GRP):
-        y_remote(across(i), 0, grp).wait_recv()
-    token = ysend[GRP - 1]
-    for i in range(1, GRP):
-        token = token + ybuf[across(i)]
+            for token in range(PAIR):
+                y_remote(quarter, token, owner_of(quarter)).start()
+    y_remote(GRP - 1, 1 - core, grp).start()
+    ybuf[mine] = ysend[GRP - 1, core]
+
+    def others(ref):
+        most = ref.at[pl.ds(0, GRP * PAIR - 1)]
+        return pltpu.make_async_remote_copy(
+            src_ref=most, dst_ref=most, send_sem=y_send, recv_sem=y_recv,
+            device_id={"seq": me}, device_id_type=MESH,
+        )
+
+    others(ybuf).wait_recv()
+    token = ybuf[0]
+    for i in range(1, GRP * PAIR):
+        token = token + ybuf[i]
     for n in range(COLS // 128):
         out_ref[0:1, n * 128 : (n + 1) * 128] = token[n : n + 1, :].astype(out_ref.dtype)
 
+    others(ybuf).wait_send()
     all_but_one(qbuf, q_send, q_recv.at[0]).wait_send()
     all_but_one(parts, p_send, p_recv).wait_send()
     all_but_one(stats, s_send, s_recv).wait_send()
-    for quarter in range(GRP - 1):
-        y_remote(grp, quarter, owner_of(quarter)).wait_send()
 
 
 def per_device(new_queries, stored_keys, stored_values, used_length, out_weight):
@@ -244,7 +268,7 @@
         scratch_shapes=[
             pltpu.VMEM((SEQ, HEADS, STRETCH, HEAD), jnp.bfloat16),
             pltpu.VMEM((SEQ, HEADS, STRETCH, HEAD), jnp.bfloat16),
-            pltpu.VMEM((GRP, HEADS, GROUP, HEAD, COLS), jnp.bfloat16),
+            pltpu.VMEM((GRP, GROUP, HEAD, COLS), jnp.bfloat16),
             pltpu.VMEM((SEQ, HEADS, GROUP, HEAD), jnp.bfloat16),
             pltpu.SMEM((SEQ,), jnp.int32),
             pltpu.VMEM((2, UNIT, ROWS, STRETCH), jnp.float32),
@@ -253,11 +277,11 @@
             pltpu.VMEM((SEQ, ROWS, HEAD), jnp.float32),
             pltpu.VMEM((SEQ, 1, 128), jnp.float32),
             pltpu.VMEM((ROWS, HEAD), jnp.float32),
-            pltpu.VMEM((GRP, COLS // 128, 128), jnp.float32),
-            pltpu.VMEM((GRP, COLS // 128, 128), jnp.float32),
+            pltpu.VMEM((GRP, PAIR, COLS // 128, 128), jnp.float32),
+            pltpu.VMEM((GRP * PAIR, COLS // 128, 128), jnp.float32),
             dma((2,)), dma((STEPS,)), dma((STEPS,)), dma((GRP,)),
             dma(()), dma((SEQ,)), dma(()), dma(()), dma(()), dma(()),
-            dma((GRP,)), dma((GRP,)),
+            dma(()), dma(()),
         ],
         compiler_params=pltpu.CompilerParams(
             collective_id=0, has_side_effects=True, vmem_limit_bytes=60 * 1024 * 1024

time: 30.2 us -> 26.2 us (0.87)
  the two profiles are of different devices: /device:TPU:96 before, /device:TPU:1 now
where the time goes in v3:
time: 26.2 us; the launch traced here: 25.7 us
  Pallas kernels  25.1 us (96%)
  local copies, waits for them, and re-layouts  0.6 us (2%)
    pallas_call x1, Pallas kernels, per_device(): pl.pallas_call(kernel, out_shape=pltpu.VMEM((1, COLS), jnp.bfloat16), in_...  25.1 us
    unnamed x1, local copies, waits for them, and re-layouts  0.6 us

profile of v3, /device:TPU:1, one launch (start us, length us, event | category | flops | bytes accessed | tf_op | source)
XLA Modules:
  0.0 25.7 jit_solution(8509722317136037432)
XLA Ops:
  0.0 25.1 %decode.1 = bf16[1,1280]{1,0:T(2,128)(2,1)S(1)} custom-call(bf16[1,2,8,128]{3,2,1,0:T(8,128)(2,1)} %q_hbm.1, bf16[32,2,512,128]{3,2,1,0:T(8,128)(2,1)} %k_hbm.1, bf16[32,2,512,128]{3,2,1,0:T(8,128)(2,1)} %v_hbm.1, s32[32]{0:T(128)} %len_hbm.1, bf16[2,8,128,5120]{3,2,1,0:T(8,128)(2,1)} %w_hbm.1), custom_call_target="tpu_custom_call" | custom-call | tf_op jit(solution)/shard_map/decode/pallas_call | solution.py:263
  25.1 0.6 %copy.7 = bf16[1,1280]{1,0:T(2,128)(2,1)} copy(bf16[1,1280]{1,0:T(2,128)(2,1)S(1)} %decode.1) | data formatting | bytes 5120

commit v4 on v3

--- a/solution.py
+++ b/solution.py
@@ -25,25 +25,20 @@
     me = lax.axis_index("seq")
     grp = lax.axis_index("group")
     layer, place = lax.div(me, ROW), lax.rem(me, ROW)
-    first = layer * ROW
-
-    def mate(i):
-        return first + lax.rem(place + i, ROW)
-
-    def column(i):
-        return lax.rem(layer + i, LAYERS) * ROW + place
+    lane_x, core = lax.div(place, PAIR), lax.rem(place, PAIR)
+    chip = me - core
+    far_first = (2, 3, 1, 0)
+    layers = {i: lax.rem(layer + i, LAYERS) * ROW for i in far_first}
+    places = {i: lax.rem(lane_x + i, ROW // PAIR) * PAIR for i in far_first}
+    peers = [layers[z] + places[x] + c for z in far_first for x in far_first if z or x for c in range(PAIR)]
+    peers.append(chip + 1 - core)
 
     def across(i):
         return lax.rem(grp + i, GRP)
 
-    core = lax.rem(me, PAIR)
-    chip = me - core
-
     barrier = pltpu.get_barrier_semaphore()
-    for i in range(1, LAYERS):
-        pl.semaphore_signal(barrier, 1, device_id={"seq": column(i)}, device_id_type=MESH)
-    for i in range(1, ROW):
-        pl.semaphore_signal(barrier, 1, device_id={"seq": mate(i)}, device_id_type=MESH)
+    for peer in peers:
+        pl.semaphore_signal(barrier, 1, device_id={"seq": peer}, device_id_type=MESH)
     for i in range(1, GRP):
         for other in range(PAIR):
             there = {"seq": chip + other, "group": across(i)}
@@ -63,7 +58,7 @@
         return pltpu.make_async_copy(v_hbm.at[some], vbuf.at[some], v_sem.at[step])
 
     def owner_of(quarter):
-        return across((2, 1, 3, 0)[quarter])
+        return across((1, 2, 3, 0)[quarter])
 
     def w_copy(quarter):
         start = pl.multiple_of(owner_of(quarter) * COLS, 128)
@@ -77,39 +72,40 @@
     for quarter in range(GRP):
         w_copy(quarter).start(priority=1)
 
-    def q_remote(source, peer):
-        return pltpu.make_async_remote_copy(
-            src_ref=qbuf.at[source], dst_ref=qbuf.at[source],
-            send_sem=q_send, recv_sem=q_recv.at[source],
+    def q_remote(peer):
+        return pltpu.make_async_remote_copy(
+            src_ref=qbuf.at[me], dst_ref=qbuf.at[me],
+            send_sem=q_send, recv_sem=q_recv.at[lax.div(me, UNIT)],
             device_id={"seq": peer}, device_id_type=MESH,
+        )
+
+    def q_wait(step, count):
+        some = qbuf.at[pl.ds(step * UNIT, count)]
+        return pltpu.make_async_remote_copy(
+            src_ref=some, dst_ref=some, send_sem=q_send, recv_sem=q_recv.at[step],
+            device_id={"seq": me}, device_id_type=MESH,
         )
 
     q_copy.wait()
     len_copy.wait()
-    pl.semaphore_wait(barrier, LAYERS - 1 + ROW - 1 + PAIR * (GRP - 1))
-    for i in range(1, LAYERS):
-        q_remote(me, column(i)).start()
-    for i in range(1, ROW):
-        q_remote(me, mate(i)).start()
-
-    @pl.loop(0, LAYERS)
-    def _(i):
-        source = i * ROW + place
-
-        @pl.when(i != layer)
+    pl.semaphore_wait(barrier, SEQ - 1 + PAIR * (GRP - 1))
+    for peer in peers:
+        q_remote(peer).start()
+
+    def arrived(step):
+        own = lax.div(me, UNIT) == step
+
+        @pl.when(own)
         def _():
-            q_remote(source, me).wait_recv()
-            for other in range(1, ROW):
-                q_remote(source, mate(other)).start()
+            q_wait(step, UNIT - 1).wait_recv()
+
+        @pl.when(jnp.logical_not(own))
+        def _():
+            q_wait(step, UNIT).wait_recv()
+
+        k_copy(step).wait()
 
     def scores(step, slot):
-        for u in range(UNIT):
-
-            @pl.when(lax.rem(step * UNIT + u, ROW) != place)
-            def _():
-                q_remote(step * UNIT + u, me).wait_recv()
-
-        k_copy(step).wait()
         lane = lax.broadcasted_iota(jnp.int32, (ROWS, STRETCH), 1) + me * STRETCH
         for u in range(UNIT):
             b = step * UNIT + u
@@ -128,7 +124,6 @@
     def reads(step, slot):
         row = lax.broadcasted_iota(jnp.int32, (ROWS, HEAD), 0)
         lane = lax.broadcasted_iota(jnp.int32, (ROWS, HEAD), 1)
-        v_copy(step).wait()
         results = []
         for u in range(UNIT):
             b = step * UNIT + u
@@ -175,15 +170,24 @@
                 s_remote(b).start()
                 p_remote(b).start()
 
+    def both(step, slot):
+        arrived(step + 1)
+        v_copy(step).wait()
+        reads(step, slot)
+        scores(step + 1, 1 - slot)
+        send(step)
+
+    arrived(0)
     scores(0, 0)
 
-    @pl.loop(0, STEPS - 1)
-    def _(step):
-        scores(step + 1, lax.rem(step + 1, 2))
-        reads(step, lax.rem(step, 2))
-        send(step)
-
-    reads(STEPS - 1, (STEPS - 1) % 2)
+    @pl.loop(0, STEPS // 2 - 1)
+    def _(i):
+        both(2 * i, 0)
+        both(2 * i + 1, 1)
+
+    both(STEPS - 2, 0)
+    v_copy(STEPS - 1).wait()
+    reads(STEPS - 1, 1)
     send(STEPS - 1)
     parts[me] = psend[me]
     stats[me] = ssend[me]
@@ -280,7 +284,7 @@
             pltpu.VMEM((GRP, PAIR, COLS // 128, 128), jnp.float32),
             pltpu.VMEM((GRP * PAIR, COLS // 128, 128), jnp.float32),
             dma((2,)), dma((STEPS,)), dma((STEPS,)), dma((GRP,)),
-            dma(()), dma((SEQ,)), dma(()), dma(()), dma(()), dma(()),
+            dma(()), dma((STEPS,)), dma(()), dma(()), dma(()), dma(()),
             dma(()), dma(()),
         ],
         compiler_params=pltpu.CompilerParams(

time: 26.2 us -> 25.5 us (0.973)
  the two profiles are of different devices: /device:TPU:1 before, /device:TPU:97 now
where the time goes in v4:
time: 25.5 us; the launch traced here: 25.4 us
  Pallas kernels  24.8 us (97%)
  local copies, waits for them, and re-layouts  0.6 us (2%)
    pallas_call x1, Pallas kernels, per_device(): pl.pallas_call(kernel, out_shape=pltpu.VMEM((1, COLS), jnp.bfloat16), in_...  24.8 us
    unnamed x1, local copies, waits for them, and re-layouts  0.6 us

profile of v4, /device:TPU:97, one launch (start us, length us, event | category | flops | bytes accessed | tf_op | source)
XLA Modules:
  0.0 25.4 jit_solution(627445044678403528)
XLA Ops:
  0.0 24.8 %decode.1 = bf16[1,1280]{1,0:T(2,128)(2,1)S(1)} custom-call(bf16[1,2,8,128]{3,2,1,0:T(8,128)(2,1)} %q_hbm.1, bf16[32,2,512,128]{3,2,1,0:T(8,128)(2,1)} %k_hbm.1, bf16[32,2,512,128]{3,2,1,0:T(8,128)(2,1)} %v_hbm.1, s32[32]{0:T(128)} %len_hbm.1, bf16[2,8,128,5120]{3,2,1,0:T(8,128)(2,1)} %w_hbm.1), custom_call_target="tpu_custom_call" | custom-call | tf_op jit(solution)/shard_map/decode/pallas_call | solution.py:267
  24.8 0.6 %copy.7 = bf16[1,1280]{1,0:T(2,128)(2,1)} copy(bf16[1,1280]{1,0:T(2,128)(2,1)S(1)} %decode.1) | data formatting | bytes 5120

commit v5 on v4

--- a/solution.py
+++ b/solution.py
@@ -7,7 +7,7 @@
 
 MESH = pl.DeviceIdType.MESH
 SEQ, GRP = 32, 4
-LAYERS, ROW, PAIR = 4, 8, 2
+ROW, PAIR = 8, 2
 HEADS, GROUP, HEAD = 2, 8, 128
 ROWS = HEADS * GROUP
 STRETCH = 512
@@ -24,21 +24,19 @@
 ):
     me = lax.axis_index("seq")
     grp = lax.axis_index("group")
-    layer, place = lax.div(me, ROW), lax.rem(me, ROW)
-    lane_x, core = lax.div(place, PAIR), lax.rem(place, PAIR)
+    core = lax.rem(me, PAIR)
     chip = me - core
-    far_first = (2, 3, 1, 0)
-    layers = {i: lax.rem(layer + i, LAYERS) * ROW for i in far_first}
-    places = {i: lax.rem(lane_x + i, ROW // PAIR) * PAIR for i in far_first}
-    peers = [layers[z] + places[x] + c for z in far_first for x in far_first if z or x for c in range(PAIR)]
-    peers.append(chip + 1 - core)
 
     def across(i):
         return lax.rem(grp + i, GRP)
 
     barrier = pltpu.get_barrier_semaphore()
-    for peer in peers:
-        pl.semaphore_signal(barrier, 1, device_id={"seq": peer}, device_id_type=MESH)
+    for peer in range(SEQ):
+
+        @pl.when(peer != me)
+        def _():
+            pl.semaphore_signal(barrier, 1, device_id={"seq": peer}, device_id_type=MESH)
+
     for i in range(1, GRP):
         for other in range(PAIR):
             there = {"seq": chip + other, "group": across(i)}
@@ -89,8 +87,13 @@
     q_copy.wait()
     len_copy.wait()
     pl.semaphore_wait(barrier, SEQ - 1 + PAIR * (GRP - 1))
-    for peer in peers:
-        q_remote(peer).start()
+    for z in (3, 2, 1, 0):
+        for x in (2, 3, 1, 0):
+            for peer in range(z * ROW + x * PAIR, z * ROW + x * PAIR + PAIR):
+
+                @pl.when(peer != me)
+                def _():
+                    q_remote(peer).start()
 
     def arrived(step):
         own = lax.div(me, UNIT) == step
@@ -170,29 +173,34 @@
                 s_remote(b).start()
                 p_remote(b).start()
 
-    def both(step, slot):
-        arrived(step + 1)
-        v_copy(step).wait()
-        reads(step, slot)
-        scores(step + 1, 1 - slot)
-        send(step)
-
     arrived(0)
     scores(0, 0)
+    arrived(1)
+    v_copy(0).wait()
+    scores(1, 1)
+    reads(0, 0)
+    send(0)
 
     @pl.loop(0, STEPS // 2 - 1)
     def _(i):
-        both(2 * i, 0)
-        both(2 * i + 1, 1)
-
-    both(STEPS - 2, 0)
+        step = 2 * i + 1
+        for ahead in range(PAIR):
+            arrived(step + 1 + ahead)
+            v_copy(step + ahead).wait()
+        scores(step + 1, 0)
+        reads(step, 1)
+        scores(step + 2, 1)
+        reads(step + 1, 0)
+        send(step)
+        send(step + 1)
+
     v_copy(STEPS - 1).wait()
+    for quarter in range(GRP):
+        w_copy(quarter).wait()
     reads(STEPS - 1, 1)
     send(STEPS - 1)
     parts[me] = psend[me]
     stats[me] = ssend[me]
-    for quarter in range(GRP):
-        w_copy(quarter).wait()
 
     def all_but_one(ref, send_sem, recv_sem):
         most = ref.at[pl.ds(0, SEQ - 1)]

time: 25.5 us -> 25.2 us (0.988)
  the two profiles are of different devices: /device:TPU:97 before, /device:TPU:1 now
where the time goes in v5:
time: 25.2 us; the launch traced here: 25.1 us
  Pallas kernels  24.5 us (97%)
  local copies, waits for them, and re-layouts  0.6 us (2%)
    pallas_call x1, Pallas kernels, per_device(): pl.pallas_call(kernel, out_shape=pltpu.VMEM((1, COLS), jnp.bfloat16), in_...  24.5 us
    unnamed x1, local copies, waits for them, and re-layouts  0.6 us

profile of v5, /device:TPU:1, one launch (start us, length us, event | category | flops | bytes accessed | tf_op | source)
XLA Modules:
  0.0 25.1 jit_solution(7596362835903035724)
XLA Ops:
  0.0 24.5 %decode.1 = bf16[1,1280]{1,0:T(2,128)(2,1)S(1)} custom-call(bf16[1,2,8,128]{3,2,1,0:T(8,128)(2,1)} %q_hbm.1, bf16[32,2,512,128]{3,2,1,0:T(8,128)(2,1)} %k_hbm.1, bf16[32,2,512,128]{3,2,1,0:T(8,128)(2,1)} %v_hbm.1, s32[32]{0:T(128)} %len_hbm.1, bf16[2,8,128,5120]{3,2,1,0:T(8,128)(2,1)} %w_hbm.1), custom_call_target="tpu_custom_call" | custom-call | tf_op jit(solution)/shard_map/decode/pallas_call | solution.py:275
  24.5 0.6 %copy.7 = bf16[1,1280]{1,0:T(2,128)(2,1)} copy(bf16[1,1280]{1,0:T(2,128)(2,1)S(1)} %decode.1) | data formatting | bytes 5120

commit v6 on v5

--- a/solution.py
+++ b/solution.py
@@ -47,40 +47,40 @@
     q_copy.start()
     len_copy.start()
 
-    def k_copy(step):
-        some = pl.ds(step * UNIT, UNIT)
-        return pltpu.make_async_copy(k_hbm.at[some], kbuf.at[some], k_sem.at[step])
-
-    def v_copy(step):
-        some = pl.ds(step * UNIT, UNIT)
-        return pltpu.make_async_copy(v_hbm.at[some], vbuf.at[some], v_sem.at[step])
+    def k_copy(layer):
+        some = pl.ds(layer * ROW, ROW)
+        return pltpu.make_async_copy(k_hbm.at[some], kbuf.at[some], k_sem.at[layer])
+
+    def v_copy(layer):
+        some = pl.ds(layer * ROW, ROW)
+        return pltpu.make_async_copy(v_hbm.at[some], vbuf.at[some], v_sem.at[layer])
 
     def owner_of(quarter):
-        return across((1, 2, 3, 0)[quarter])
+        return quarter + (quarter >= grp).astype(jnp.int32) if quarter < GRP - 1 else grp
 
     def w_copy(quarter):
         start = pl.multiple_of(owner_of(quarter) * COLS, 128)
         return pltpu.make_async_copy(
-            w_hbm.at[core, :, :, pl.ds(start, COLS)], wbuf.at[quarter], w_sem.at[quarter]
-        )
-
-    for step in range(STEPS):
-        k_copy(step).start(priority=1)
-        v_copy(step).start(priority=1)
+            w_hbm.at[core, :, :, pl.ds(start, COLS)], wbuf.at[quarter], w_sem.at[0]
+        )
+
+    for layer in range(SEQ // ROW):
+        k_copy(layer).start(priority=1)
+        v_copy(layer).start(priority=1)
     for quarter in range(GRP):
         w_copy(quarter).start(priority=1)
 
     def q_remote(peer):
         return pltpu.make_async_remote_copy(
             src_ref=qbuf.at[me], dst_ref=qbuf.at[me],
-            send_sem=q_send, recv_sem=q_recv.at[lax.div(me, UNIT)],
+            send_sem=q_send, recv_sem=q_recv.at[lax.div(me, PAIR)],
             device_id={"seq": peer}, device_id_type=MESH,
         )
 
-    def q_wait(step, count):
-        some = qbuf.at[pl.ds(step * UNIT, count)]
-        return pltpu.make_async_remote_copy(
-            src_ref=some, dst_ref=some, send_sem=q_send, recv_sem=q_recv.at[step],
+    def q_wait(place, count):
+        some = qbuf.at[pl.ds(place * PAIR, count)]
+        return pltpu.make_async_remote_copy(
+            src_ref=some, dst_ref=some, send_sem=q_send, recv_sem=q_recv.at[place],
             device_id={"seq": me}, device_id_type=MESH,
         )
 
@@ -95,22 +95,20 @@
                 def _():
                     q_remote(peer).start()
 
-    def arrived(step):
-        own = lax.div(me, UNIT) == step
+    def arrived(place):
+        own = place * PAIR == chip
 
         @pl.when(own)
         def _():
-            q_wait(step, UNIT - 1).wait_recv()
+            q_wait(place, PAIR - 1).wait_recv()
 
         @pl.when(jnp.logical_not(own))
         def _():
-            q_wait(step, UNIT).wait_recv()
-
-        k_copy(step).wait()
-
-    def scores(step, slot):
+            q_wait(place, PAIR).wait_recv()
+
+    def scores(step, slot, units=range(UNIT)):
         lane = lax.broadcasted_iota(jnp.int32, (ROWS, STRETCH), 1) + me * STRETCH
-        for u in range(UNIT):
+        for u in units:
             b = step * UNIT + u
             zero = jnp.zeros((GROUP, HEAD), jnp.float32)
             q0 = qbuf[b, 0].astype(jnp.float32)
@@ -124,11 +122,11 @@
             )
             logits[slot, u] = jnp.where(lane < lens[b], logit, -1e30)
 
-    def reads(step, slot):
+    def reads(step, slot, units=range(UNIT)):
         row = lax.broadcasted_iota(jnp.int32, (ROWS, HEAD), 0)
         lane = lax.broadcasted_iota(jnp.int32, (ROWS, HEAD), 1)
         results = []
-        for u in range(UNIT):
+        for u in units:
             b = step * UNIT + u
             logit = logits[slot, u]
             top = jnp.max(logit, axis=1, keepdims=True)
@@ -141,11 +139,11 @@
                 jnp.concatenate([high, low], axis=0), v, preferred_element_type=jnp.float32
             )
             results.append((both[:ROWS] + both[ROWS:], top, total))
-        for u in range(0, UNIT, PAIR):
+        for n, u in enumerate(units[::PAIR]):
             for head in range(HEADS):
                 own = slice(head * GROUP, (head + 1) * GROUP)
                 here = slice(head * HEAD, (head + 1) * HEAD)
-                two = results[u : u + PAIR]
+                two = results[n * PAIR : (n + 1) * PAIR]
                 top = jnp.concatenate([r[1][own] for r in two], axis=0)
                 total = jnp.concatenate([r[2][own] for r in two], axis=0)
                 psend[step * UNIT + u + head] = jnp.concatenate([r[0][own, here] for r in two], axis=0)
@@ -164,8 +162,8 @@
             device_id={"seq": b}, device_id_type=MESH,
         )
 
-    def send(step):
-        for u in range(UNIT):
+    def send(step, units=range(UNIT)):
+        for u in units:
             b = step * UNIT + u
 
             @pl.when(b != me)
@@ -173,20 +171,28 @@
                 s_remote(b).start()
                 p_remote(b).start()
 
+    head, tail = range(PAIR), range(PAIR, UNIT)
     arrived(0)
-    scores(0, 0)
+    k_copy(0).wait()
+    v_copy(0).wait()
+    scores(0, 0, head)
+    reads(0, 0, head)
+    send(0, head)
     arrived(1)
-    v_copy(0).wait()
+    arrived(2)
+    arrived(3)
+    scores(0, 0, tail)
     scores(1, 1)
-    reads(0, 0)
-    send(0)
-
-    @pl.loop(0, STEPS // 2 - 1)
-    def _(i):
-        step = 2 * i + 1
-        for ahead in range(PAIR):
-            arrived(step + 1 + ahead)
-            v_copy(step + ahead).wait()
+    reads(0, 0, tail)
+    send(0, tail)
+
+    @pl.loop(0, SEQ // ROW - 1)
+    def _(layer):
+        step = 2 * layer + 1
+        for i in range(4):
+            arrived(2 * (step + 1) + i)
+        k_copy(layer + 1).wait()
+        v_copy(layer + 1).wait()
         scores(step + 1, 0)
         reads(step, 1)
         scores(step + 2, 1)
@@ -194,9 +200,7 @@
         send(step)
         send(step + 1)
 
-    v_copy(STEPS - 1).wait()
-    for quarter in range(GRP):
-        w_copy(quarter).wait()
+    pltpu.make_async_copy(wbuf, wbuf, w_sem.at[0]).wait()
     reads(STEPS - 1, 1)
     send(STEPS - 1)
     parts[me] = psend[me]
@@ -236,16 +240,28 @@
             device_id={"seq": chip + token, "group": peer}, device_id_type=MESH,
         )
 
+    def term(quarter, start, stop, top=0, bottom=GROUP):
+        return jnp.dot(
+            spread[:, top * HEAD : bottom * HEAD],
+            wbuf[quarter, top:bottom, :, start:stop].reshape((bottom - top) * HEAD, stop - start),
+            preferred_element_type=jnp.float32,
+        )
+
+    def rest(quarter):
+        last = term(quarter, 1024, COLS, 0, GROUP // 2) + term(quarter, 1024, COLS, GROUP // 2)
+        return [term(quarter, 512, 1024), last]
+
+    terms = [term(0, 0, 512), *rest(0)]
     for quarter in range(GRP):
-        term = jnp.dot(
-            spread, wbuf[quarter].reshape(GROUP * HEAD, COLS), preferred_element_type=jnp.float32
-        )
+        ahead = [term(quarter + 1, 0, 512)] if quarter < GRP - 1 else []
+        line = jnp.concatenate(terms, axis=1)
         for token in range(PAIR):
             for n in range(COLS // 128):
-                ysend[quarter, token, n : n + 1, :] = term[token : token + 1, n * 128 : (n + 1) * 128]
+                ysend[quarter, token, n : n + 1, :] = line[token : token + 1, n * 128 : (n + 1) * 128]
         if quarter < GRP - 1:
             for token in range(PAIR):
                 y_remote(quarter, token, owner_of(quarter)).start()
+            terms = [*ahead, *rest(quarter + 1)]
     y_remote(GRP - 1, 1 - core, grp).start()
     ybuf[mine] = ysend[GRP - 1, core]
 
@@ -291,8 +307,8 @@
             pltpu.VMEM((ROWS, HEAD), jnp.float32),
             pltpu.VMEM((GRP, PAIR, COLS // 128, 128), jnp.float32),
             pltpu.VMEM((GRP * PAIR, COLS // 128, 128), jnp.float32),
-            dma((2,)), dma((STEPS,)), dma((STEPS,)), dma((GRP,)),
-            dma(()), dma((STEPS,)), dma(()), dma(()), dma(()), dma(()),
+            dma((2,)), dma((SEQ // ROW,)), dma((SEQ // ROW,)), dma((1,)),
+            dma(()), dma((SEQ // PAIR,)), dma(()), dma(()), dma(()), dma(()),
             dma(()), dma(()),
         ],
         compiler_params=pltpu.CompilerParams(

time: 25.2 us -> 24.7 us (0.980)
  the two profiles are of different devices: /device:TPU:1 before, /device:TPU:97 now
where the time goes in v6:
time: 24.7 us; the launch traced here: 24.6 us
  Pallas kernels  24 us (97%)
  local copies, waits for them, and re-layouts  0.6 us (2%)
    pallas_call x1, Pallas kernels, per_device(): pl.pallas_call(kernel, out_shape=pltpu.VMEM((1, COLS), jnp.bfloat16), in_...  24 us
    unnamed x1, local copies, waits for them, and re-layouts  0.6 us

profile of v6, /device:TPU:97, one launch (start us, length us, event | category | flops | bytes accessed | tf_op | source)
XLA Modules:
  0.0 24.6 jit_solution(3109343537876294251)
XLA Ops:
  0.0 24.0 %decode.1 = bf16[1,1280]{1,0:T(2,128)(2,1)S(1)} custom-call(bf16[1,2,8,128]{3,2,1,0:T(8,128)(2,1)} %q_hbm.1, bf16[32,2,512,128]{3,2,1,0:T(8,128)(2,1)} %k_hbm.1, bf16[32,2,512,128]{3,2,1,0:T(8,128)(2,1)} %v_hbm.1, s32[32]{0:T(128)} %len_hbm.1, bf16[2,8,128,5120]{3,2,1,0:T(8,128)(2,1)} %w_hbm.1), custom_call_target="tpu_custom_call" | custom-call | tf_op jit(solution)/shard_map/decode/pallas_call | solution.py:291
  24.0 0.6 %copy.7 = bf16[1,1280]{1,0:T(2,128)(2,1)} copy(bf16[1,1280]{1,0:T(2,128)(2,1)S(1)} %decode.1) | data formatting | bytes 5120

commit v7 on v6

--- a/solution.py
+++ b/solution.py
@@ -20,7 +20,7 @@
 def kernel(
     q_hbm, k_hbm, v_hbm, len_hbm, w_hbm, out_ref,
     kbuf, vbuf, wbuf, qbuf, lens, logits, psend, ssend, parts, stats, rows, ysend, ybuf,
-    local_sem, k_sem, v_sem, w_sem, q_send, q_recv, p_send, p_recv, s_send, s_recv, y_send, y_recv,
+    local_sem, kv_sem, w_sem, q_send, q_recv, p_send, p_recv, s_send, s_recv, y_send, y_recv,
 ):
     me = lax.axis_index("seq")
     grp = lax.axis_index("group")
@@ -47,13 +47,19 @@
     q_copy.start()
     len_copy.start()
 
-    def k_copy(layer):
-        some = pl.ds(layer * ROW, ROW)
-        return pltpu.make_async_copy(k_hbm.at[some], kbuf.at[some], k_sem.at[layer])
-
-    def v_copy(layer):
-        some = pl.ds(layer * ROW, ROW)
-        return pltpu.make_async_copy(v_hbm.at[some], vbuf.at[some], v_sem.at[layer])
+    def nth(n):
+        if isinstance(n, int):
+            return {3: 6, 4: 3, 5: 4, 6: 5}.get(n, n)
+        return n + jnp.where(n == 3, 3, 0) + jnp.where(n == 4, -1, 0) + jnp.where(n == 5, -1, 0) + jnp.where(n == 6, -1, 0)
+
+    def load(n):
+        some = pl.ds(nth(n) * UNIT, UNIT)
+        pltpu.make_async_copy(k_hbm.at[some], kbuf.at[some], kv_sem.at[n]).start(priority=1)
+        pltpu.make_async_copy(v_hbm.at[some], vbuf.at[some], kv_sem.at[n]).start(priority=1)
+
+    def loaded(n):
+        both = kbuf.at[pl.ds(0, 2 * UNIT)]
+        pltpu.make_async_copy(both, both, kv_sem.at[n]).wait()
 
     def owner_of(quarter):
         return quarter + (quarter >= grp).astype(jnp.int32) if quarter < GRP - 1 else grp
@@ -64,9 +70,8 @@
             w_hbm.at[core, :, :, pl.ds(start, COLS)], wbuf.at[quarter], w_sem.at[0]
         )
 
-    for layer in range(SEQ // ROW):
-        k_copy(layer).start(priority=1)
-        v_copy(layer).start(priority=1)
+    for n in range(STEPS):
+        load(n)
     for quarter in range(GRP):
         w_copy(quarter).start(priority=1)
 
@@ -173,36 +178,38 @@
 
     head, tail = range(PAIR), range(PAIR, UNIT)
     arrived(0)
-    k_copy(0).wait()
-    v_copy(0).wait()
+    loaded(0)
     scores(0, 0, head)
     reads(0, 0, head)
     send(0, head)
     arrived(1)
-    arrived(2)
-    arrived(3)
+    arrived(2 * nth(1))
+    arrived(2 * nth(1) + 1)
+    loaded(1)
     scores(0, 0, tail)
-    scores(1, 1)
+    scores(nth(1), 1)
     reads(0, 0, tail)
     send(0, tail)
 
-    @pl.loop(0, SEQ // ROW - 1)
-    def _(layer):
-        step = 2 * layer + 1
-        for i in range(4):
-            arrived(2 * (step + 1) + i)
-        k_copy(layer + 1).wait()
-        v_copy(layer + 1).wait()
-        scores(step + 1, 0)
-        reads(step, 1)
-        scores(step + 2, 1)
-        reads(step + 1, 0)
-        send(step)
-        send(step + 1)
+    @pl.loop(0, STEPS // 2 - 1)
+    def _(i):
+        n = 2 * i + 1
+        now, second, third = nth(n), nth(n + 1), nth(n + 2)
+        for step in (second, third):
+            arrived(2 * step)
+            arrived(2 * step + 1)
+        loaded(n + 1)
+        loaded(n + 2)
+        scores(second, 0)
+        reads(now, 1)
+        scores(third, 1)
+        reads(second, 0)
+        send(now)
+        send(second)
 
     pltpu.make_async_copy(wbuf, wbuf, w_sem.at[0]).wait()
-    reads(STEPS - 1, 1)
-    send(STEPS - 1)
+    reads(nth(STEPS - 1), 1)
+    send(nth(STEPS - 1))
     parts[me] = psend[me]
     stats[me] = ssend[me]
 
@@ -240,20 +247,11 @@
             device_id={"seq": chip + token, "group": peer}, device_id_type=MESH,
         )
 
-    def term(quarter, start, stop, top=0, bottom=GROUP):
-        return jnp.dot(
-            spread[:, top * HEAD : bottom * HEAD],
-            wbuf[quarter, top:bottom, :, start:stop].reshape((bottom - top) * HEAD, stop - start),
-            preferred_element_type=jnp.float32,
-        )
-
-    def rest(quarter):
-        last = term(quarter, 1024, COLS, 0, GROUP // 2) + term(quarter, 1024, COLS, GROUP // 2)
-        return [term(quarter, 512, 1024), last]
-
-    terms = [term(0, 0, 512), *rest(0)]
-    for quarter in range(GRP):
-        ahead = [term(quarter + 1, 0, 512)] if quarter < GRP - 1 else []
+    def part(*where):
+        w = [wbuf[q, :, :, 256 * a : 256 * b].reshape(GROUP * HEAD, 256 * (b - a)) for q, a, b in where]
+        return jnp.dot(spread, jnp.concatenate(w, axis=1), preferred_element_type=jnp.float32)
+
+    def ship(quarter, terms):
         line = jnp.concatenate(terms, axis=1)
         for token in range(PAIR):
             for n in range(COLS // 128):
@@ -261,7 +259,17 @@
         if quarter < GRP - 1:
             for token in range(PAIR):
                 y_remote(quarter, token, owner_of(quarter)).start()
-            terms = [*ahead, *rest(quarter + 1)]
+
+    first, second, shared = part((0, 0, 2)), part((0, 2, 4)), part((0, 4, 5), (1, 0, 1))
+    ahead = part((1, 1, 3))
+    ship(0, [first, second, shared[:, :256]])
+    third = part((1, 3, 5))
+    first = part((2, 0, 2))
+    ship(1, [shared[:, 256:], ahead, third])
+    second, shared = part((2, 2, 4)), part((2, 4, 5), (3, 0, 1))
+    ahead = part((3, 1, 3))
+    ship(2, [first, second, shared[:, :256]])
+    ship(3, [shared[:, 256:], ahead, part((3, 3, 5))])
     y_remote(GRP - 1, 1 - core, grp).start()
     ybuf[mine] = ysend[GRP - 1, core]
 
@@ -307,7 +315,7 @@
             pltpu.VMEM((ROWS, HEAD), jnp.float32),
             pltpu.VMEM((GRP, PAIR, COLS // 128, 128), jnp.float32),
             pltpu.VMEM((GRP * PAIR, COLS // 128, 128), jnp.float32),
-            dma((2,)), dma((SEQ // ROW,)), dma((SEQ // ROW,)), dma((1,)),
+            dma((2,)), dma((STEPS,)), dma((1,)),
             dma(()), dma((SEQ // PAIR,)), dma(()), dma(()), dma(()), dma(()),
             dma(()), dma(()),
         ],

time: 24.7 us -> 24.3 us (0.984)
  the two profiles are of different devices: /device:TPU:97 before, /device:TPU:1 now
where the time goes in v7:
time: 24.3 us; the launch traced here: 24.1 us
  Pallas kernels  23.4 us (96%)
  local copies, waits for them, and re-layouts  0.6 us (2%)
    pallas_call x1, Pallas kernels, per_device(): pl.pallas_call(kernel, out_shape=pltpu.VMEM((1, COLS), jnp.bfloat16), in_...  23.4 us
    unnamed x1, local copies, waits for them, and re-layouts  0.6 us

profile of v7, /device:TPU:1, one launch (start us, length us, event | category | flops | bytes accessed | tf_op | source)
XLA Modules:
  0.0 24.1 jit_solution(3030206765162103050)
XLA Ops:
  0.0 23.4 %decode.1 = bf16[1,1280]{1,0:T(2,128)(2,1)S(1)} custom-call(bf16[1,2,8,128]{3,2,1,0:T(8,128)(2,1)} %q_hbm.1, bf16[32,2,512,128]{3,2,1,0:T(8,128)(2,1)} %k_hbm.1, bf16[32,2,512,128]{3,2,1,0:T(8,128)(2,1)} %v_hbm.1, s32[32]{0:T(128)} %len_hbm.1, bf16[2,8,128,5120]{3,2,1,0:T(8,128)(2,1)} %w_hbm.1), custom_call_target="tpu_custom_call" | custom-call | tf_op jit(solution)/shard_map/decode/pallas_call | solution.py:299
  23.5 0.6 %copy.7 = bf16[1,1280]{1,0:T(2,128)(2,1)} copy(bf16[1,1280]{1,0:T(2,128)(2,1)S(1)} %decode.1) | data formatting | bytes 5120

commit v8 on v7

--- a/solution.py
+++ b/solution.py
@@ -153,7 +153,7 @@
                 total = jnp.concatenate([r[2][own] for r in two], axis=0)
                 psend[step * UNIT + u + head] = jnp.concatenate([r[0][own, here] for r in two], axis=0)
                 pair = jnp.where(lane == row, top, jnp.where(lane == row + ROWS, total, 0.0))
-                ssend[step * UNIT + u + head] = jnp.sum(pair, axis=0, keepdims=True)
+                ssend[pl.ds(step * UNIT + u + head, 1)] = jnp.sum(pair, axis=0, keepdims=True)
 
     def p_remote(b):
         return pltpu.make_async_remote_copy(
@@ -163,7 +163,7 @@
 
     def s_remote(b):
         return pltpu.make_async_remote_copy(
-            src_ref=ssend.at[b], dst_ref=stats.at[me], send_sem=s_send, recv_sem=s_recv,
+            src_ref=ssend.at[pl.ds(b, 1)], dst_ref=stats.at[pl.ds(me, 1)], send_sem=s_send, recv_sem=s_recv,
             device_id={"seq": b}, device_id_type=MESH,
         )
 
@@ -202,16 +202,16 @@
         loaded(n + 2)
         scores(second, 0)
         reads(now, 1)
+        send(now)
         scores(third, 1)
         reads(second, 0)
-        send(now)
         send(second)
 
     pltpu.make_async_copy(wbuf, wbuf, w_sem.at[0]).wait()
     reads(nth(STEPS - 1), 1)
     send(nth(STEPS - 1))
     parts[me] = psend[me]
-    stats[me] = ssend[me]
+    stats[pl.ds(me, 1)] = ssend[pl.ds(me, 1)]
 
     def all_but_one(ref, send_sem, recv_sem):
         most = ref.at[pl.ds(0, SEQ - 1)]
@@ -221,7 +221,7 @@
         )
 
     all_but_one(stats, s_send, s_recv).wait_recv()
-    stat = stats[:, 0, :]
+    stat = stats[...]
     best = jnp.max(stat, axis=0, keepdims=True)
     scale = jnp.exp2((stat - best) * TO_EXP2)
     sums = pltpu.roll(stat, HEAD - ROWS, axis=1)
@@ -280,17 +280,16 @@
             device_id={"seq": me}, device_id_type=MESH,
         )
 
+    all_but_one(qbuf, q_send, q_recv.at[0]).wait_send()
+    all_but_one(stats, s_send, s_recv).wait_send()
+    all_but_one(parts, p_send, p_recv).wait_send()
+    others(ybuf).wait_send()
     others(ybuf).wait_recv()
     token = ybuf[0]
     for i in range(1, GRP * PAIR):
         token = token + ybuf[i]
     for n in range(COLS // 128):
         out_ref[0:1, n * 128 : (n + 1) * 128] = token[n : n + 1, :].astype(out_ref.dtype)
-
-    others(ybuf).wait_send()
-    all_but_one(qbuf, q_send, q_recv.at[0]).wait_send()
-    all_but_one(parts, p_send, p_recv).wait_send()
-    all_but_one(stats, s_send, s_recv).wait_send()
 
 
 def per_device(new_queries, stored_keys, stored_values, used_length, out_weight):
@@ -309,9 +308,9 @@
             pltpu.SMEM((SEQ,), jnp.int32),
             pltpu.VMEM((2, UNIT, ROWS, STRETCH), jnp.float32),
             pltpu.VMEM((SEQ, ROWS, HEAD), jnp.float32),
-            pltpu.VMEM((SEQ, 1, 128), jnp.float32),
+            pltpu.VMEM((SEQ, 128), jnp.float32),
             pltpu.VMEM((SEQ, ROWS, HEAD), jnp.float32),
-            pltpu.VMEM((SEQ, 1, 128), jnp.float32),
+            pltpu.VMEM((SEQ, 128), jnp.float32),
             pltpu.VMEM((ROWS, HEAD), jnp.float32),
             pltpu.VMEM((GRP, PAIR, COLS // 128, 128), jnp.float32),
             pltpu.VMEM((GRP * PAIR, COLS // 128, 128), jnp.float32),

time: 24.3 us -> 24.2 us (level)
  no operation moved by 1% of the time
where the time goes in v8:
time: 24.2 us; the launch traced here: 24 us
  Pallas kernels  23.4 us (97%)
  local copies, waits for them, and re-layouts  0.6 us (2%)
    pallas_call x1, Pallas kernels, per_device(): pl.pallas_call(kernel, out_shape=pltpu.VMEM((1, COLS), jnp.bfloat16), in_...  23.4 us
    unnamed x1, local copies, waits for them, and re-layouts  0.6 us

profile of v8, /device:TPU:1, one launch (start us, length us, event | category | flops | bytes accessed | tf_op | source)
XLA Modules:
  0.0 24.0 jit_solution(18185797646825921297)
XLA Ops:
  0.0 23.4 %decode.1 = bf16[1,1280]{1,0:T(2,128)(2,1)S(1)} custom-call(bf16[1,2,8,128]{3,2,1,0:T(8,128)(2,1)} %q_hbm.1, bf16[32,2,512,128]{3,2,1,0:T(8,128)(2,1)} %k_hbm.1, bf16[32,2,512,128]{3,2,1,0:T(8,128)(2,1)} %v_hbm.1, s32[32]{0:T(128)} %len_hbm.1, bf16[2,8,128,5120]{3,2,1,0:T(8,128)(2,1)} %w_hbm.1), custom_call_target="tpu_custom_call" | custom-call | tf_op jit(solution)/shard_map/decode/pallas_call | solution.py:298
  23.4 0.6 %copy.7 = bf16[1,1280]{1,0:T(2,128)(2,1)} copy(bf16[1,1280]{1,0:T(2,128)(2,1)S(1)} %decode.1) | data formatting | bytes 5120

commit v9 on v8

--- a/solution.py
+++ b/solution.py
@@ -234,10 +234,13 @@
         read = read + parts[i] * weight[:, i : i + 1]
     rows[...] = read.astype(jnp.bfloat16).astype(jnp.float32)
     even = lax.broadcasted_iota(jnp.int32, (GROUP, HEAD), 0) == 0
-    spread = jnp.concatenate(
+    wide = jnp.concatenate(
         [jnp.where(even, rows[r : r + 1, :], rows[GROUP + r : GROUP + r + 1, :]) for r in range(GROUP)],
         axis=1,
-    ).astype(jnp.bfloat16)
+    )
+    spread = wide.astype(jnp.bfloat16)
+    deep = GROUP * HEAD // 2
+    folded = jnp.concatenate([wide[:, :deep], wide[:, deep:]], axis=0).astype(jnp.bfloat16)
 
     mine = grp * PAIR + core
 
@@ -247,9 +250,17 @@
             device_id={"seq": chip + token, "group": peer}, device_id_type=MESH,
         )
 
-    def part(*where):
-        w = [wbuf[q, :, :, 256 * a : 256 * b].reshape(GROUP * HEAD, 256 * (b - a)) for q, a, b in where]
-        return jnp.dot(spread, jnp.concatenate(w, axis=1), preferred_element_type=jnp.float32)
+    def pair(quarter, start):
+        w = wbuf[quarter, :, :, start : start + 512].reshape(GROUP * HEAD, 512)
+        return jnp.dot(spread, w, preferred_element_type=jnp.float32)
+
+    def single(quarter):
+        w = wbuf[quarter, :, :, 1024:COLS]
+        w = jnp.concatenate(
+            [w[: GROUP // 2].reshape(deep, 256), w[GROUP // 2 :].reshape(deep, 256)], axis=1
+        )
+        both = jnp.dot(folded, w, preferred_element_type=jnp.float32)
+        return both[:GROUP, :256] + both[GROUP:, 256:]
 
     def ship(quarter, terms):
         line = jnp.concatenate(terms, axis=1)
@@ -260,16 +271,12 @@
             for token in range(PAIR):
                 y_remote(quarter, token, owner_of(quarter)).start()
 
-    first, second, shared = part((0, 0, 2)), part((0, 2, 4)), part((0, 4, 5), (1, 0, 1))
-    ahead = part((1, 1, 3))
-    ship(0, [first, second, shared[:, :256]])
-    third = part((1, 3, 5))
-    first = part((2, 0, 2))
-    ship(1, [shared[:, 256:], ahead, third])
-    second, shared = part((2, 2, 4)), part((2, 4, 5), (3, 0, 1))
-    ahead = part((3, 1, 3))
-    ship(2, [first, second, shared[:, :256]])
-    ship(3, [shared[:, 256:], ahead, part((3, 3, 5))])
+    ahead = pair(0, 0)
+    for quarter in range(GRP):
+        terms = [ahead, pair(quarter, 512), single(quarter)]
+        if quarter < GRP - 1:
+            ahead = pair(quarter + 1, 0)
+        ship(quarter, terms)
     y_remote(GRP - 1, 1 - core, grp).start()
     ybuf[mine] = ysend[GRP - 1, core]
 

time: 24.2 us -> 24.1 us (level)
  no operation moved by 1% of the time
where the time goes in v9:
time: 24.1 us; the launch traced here: 24 us
  Pallas kernels  23.4 us (97%)
  local copies, waits for them, and re-layouts  0.6 us (2%)
    pallas_call x1, Pallas kernels, per_device(): pl.pallas_call(kernel, out_shape=pltpu.VMEM((1, COLS), jnp.bfloat16), in_...  23.4 us
    unnamed x1, local copies, waits for them, and re-layouts  0.6 us

profile of v9, /device:TPU:1, one launch (start us, length us, event | category | flops | bytes accessed | tf_op | source)
XLA Modules:
  0.0 24.0 jit_solution(13020087520137853161)
XLA Ops:
  0.0 23.4 %decode.1 = bf16[1,1280]{1,0:T(2,128)(2,1)S(1)} custom-call(bf16[1,2,8,128]{3,2,1,0:T(8,128)(2,1)} %q_hbm.1, bf16[32,2,512,128]{3,2,1,0:T(8,128)(2,1)} %k_hbm.1, bf16[32,2,512,128]{3,2,1,0:T(8,128)(2,1)} %v_hbm.1, s32[32]{0:T(128)} %len_hbm.1, bf16[2,8,128,5120]{3,2,1,0:T(8,128)(2,1)} %w_hbm.1), custom_call_target="tpu_custom_call" | custom-call | tf_op jit(solution)/shard_map/decode/pallas_call | solution.py:305
  23.4 0.6 %copy.7 = bf16[1,1280]{1,0:T(2,128)(2,1)} copy(bf16[1,1280]{1,0:T(2,128)(2,1)S(1)} %decode.1) | data formatting | bytes 5120

commit v10 on v9

--- a/solution.py
+++ b/solution.py
@@ -14,6 +14,7 @@
 COLS = 1280
 UNIT = 4
 STEPS = SEQ // UNIT
+KINDS = 2
 TO_EXP2 = HEAD ** (-0.5) * 1.4426950408889634
 
 
@@ -152,8 +153,9 @@
                 top = jnp.concatenate([r[1][own] for r in two], axis=0)
                 total = jnp.concatenate([r[2][own] for r in two], axis=0)
                 psend[step * UNIT + u + head] = jnp.concatenate([r[0][own, here] for r in two], axis=0)
-                pair = jnp.where(lane == row, top, jnp.where(lane == row + ROWS, total, 0.0))
-                ssend[pl.ds(step * UNIT + u + head, 1)] = jnp.sum(pair, axis=0, keepdims=True)
+                for n_of, kind in enumerate((top, total)):
+                    line = jnp.sum(jnp.where(lane == row, kind, 0.0), axis=0, keepdims=True)
+                    ssend[pl.ds(KINDS * (step * UNIT + u + head) + n_of, 1)] = line
 
     def p_remote(b):
         return pltpu.make_async_remote_copy(
@@ -163,7 +165,7 @@
 
     def s_remote(b):
         return pltpu.make_async_remote_copy(
-            src_ref=ssend.at[pl.ds(b, 1)], dst_ref=stats.at[pl.ds(me, 1)], send_sem=s_send, recv_sem=s_recv,
+            src_ref=ssend.at[pl.ds(KINDS * b, KINDS)], dst_ref=stats.at[pl.ds(KINDS * me, KINDS)], send_sem=s_send, recv_sem=s_recv,
             device_id={"seq": b}, device_id_type=MESH,
         )
 
@@ -211,20 +213,19 @@
     reads(nth(STEPS - 1), 1)
     send(nth(STEPS - 1))
     parts[me] = psend[me]
-    stats[pl.ds(me, 1)] = ssend[pl.ds(me, 1)]
-
-    def all_but_one(ref, send_sem, recv_sem):
-        most = ref.at[pl.ds(0, SEQ - 1)]
+    for kind in range(KINDS):
+        stats[pl.ds(KINDS * me + kind, 1)] = ssend[pl.ds(KINDS * me + kind, 1)]
+
+    def all_but_one(ref, send_sem, recv_sem, each=1):
+        most = ref.at[pl.ds(0, each * (SEQ - 1))]
         return pltpu.make_async_remote_copy(
             src_ref=most, dst_ref=most, send_sem=send_sem, recv_sem=recv_sem,
             device_id={"seq": me}, device_id_type=MESH,
         )
 
-    all_but_one(stats, s_send, s_recv).wait_recv()
-    stat = stats[...]
-    best = jnp.max(stat, axis=0, keepdims=True)
-    scale = jnp.exp2((stat - best) * TO_EXP2)
-    sums = pltpu.roll(stat, HEAD - ROWS, axis=1)
+    all_but_one(stats, s_send, s_recv, KINDS).wait_recv()
+    tops, sums = (stats[pl.ds(kind, SEQ, stride=KINDS)] for kind in range(KINDS))
+    scale = jnp.exp2((tops - jnp.max(tops, axis=0, keepdims=True)) * TO_EXP2)
     weight = scale / jnp.sum(sums * scale, axis=0, keepdims=True)
     weight = weight.T[:ROWS]
 
@@ -288,7 +289,7 @@
         )
 
     all_but_one(qbuf, q_send, q_recv.at[0]).wait_send()
-    all_but_one(stats, s_send, s_recv).wait_send()
+    all_but_one(stats, s_send, s_recv, KINDS).wait_send()
     all_but_one(parts, p_send, p_recv).wait_send()
     others(ybuf).wait_send()
     others(ybuf).wait_recv()
@@ -315,9 +316,9 @@
             pltpu.SMEM((SEQ,), jnp.int32),
             pltpu.VMEM((2, UNIT, ROWS, STRETCH), jnp.float32),
             pltpu.VMEM((SEQ, ROWS, HEAD), jnp.float32),
-            pltpu.VMEM((SEQ, 128), jnp.float32),
+            pltpu.VMEM((KINDS * SEQ, 128), jnp.float32),
             pltpu.VMEM((SEQ, ROWS, HEAD), jnp.float32),
-            pltpu.VMEM((SEQ, 128), jnp.float32),
+            pltpu.VMEM((KINDS * SEQ, 128), jnp.float32),
             pltpu.VMEM((ROWS, HEAD), jnp.float32),
             pltpu.VMEM((GRP, PAIR, COLS // 128, 128), jnp.float32),
             pltpu.VMEM((GRP * PAIR, COLS // 128, 128), jnp.float32),

time: 24.1 us -> 24.1 us (level)
  no operation moved by 1% of the time
where the time goes in v10:
time: 24.1 us; the launch traced here: 23.9 us
  Pallas kernels  23.3 us (97%)
  local copies, waits for them, and re-layouts  0.6 us (2%)
    pallas_call x1, Pallas kernels, per_device(): pl.pallas_call(kernel, out_shape=pltpu.VMEM((1, COLS), jnp.bfloat16), in_...  23.3 us
    unnamed x1, local copies, waits for them, and re-layouts  0.6 us

profile of v10, /device:TPU:1, one launch (start us, length us, event | category | flops | bytes accessed | tf_op | source)
XLA Modules:
  0.0 23.9 jit_solution(11360177624712066987)
XLA Ops:
  0.0 23.3 %decode.1 = bf16[1,1280]{1,0:T(2,128)(2,1)S(1)} custom-call(bf16[1,2,8,128]{3,2,1,0:T(8,128)(2,1)} %q_hbm.1, bf16[32,2,512,128]{3,2,1,0:T(8,128)(2,1)} %k_hbm.1, bf16[32,2,512,128]{3,2,1,0:T(8,128)(2,1)} %v_hbm.1, s32[32]{0:T(128)} %len_hbm.1, bf16[2,8,128,5120]{3,2,1,0:T(8,128)(2,1)} %w_hbm.1), custom_call_target="tpu_custom_call" | custom-call | tf_op jit(solution)/shard_map/decode/pallas_call | solution.py:306
  23.3 0.6 %copy.7 = bf16[1,1280]{1,0:T(2,128)(2,1)} copy(bf16[1,1280]{1,0:T(2,128)(2,1)S(1)} %decode.1) | data formatting | bytes 5120

commit v11 on v10

--- a/solution.py
+++ b/solution.py
@@ -193,7 +193,7 @@
     reads(0, 0, tail)
     send(0, tail)
 
-    @pl.loop(0, STEPS // 2 - 1)
+    @pl.loop(0, STEPS // 2 - 2)
     def _(i):
         n = 2 * i + 1
         now, second, third = nth(n), nth(n + 1), nth(n + 2)
@@ -209,8 +209,18 @@
         reads(second, 0)
         send(second)
 
+    for n in (STEPS - 2, STEPS - 1):
+        arrived(2 * nth(n))
+        arrived(2 * nth(n) + 1)
+        loaded(n)
     pltpu.make_async_copy(wbuf, wbuf, w_sem.at[0]).wait()
+    scores(nth(STEPS - 2), 0)
+    reads(nth(STEPS - 3), 1)
+    send(nth(STEPS - 3))
+    scores(nth(STEPS - 1), 1)
+    reads(nth(STEPS - 2), 0)
     reads(nth(STEPS - 1), 1)
+    send(nth(STEPS - 2))
     send(nth(STEPS - 1))
     parts[me] = psend[me]
     for kind in range(KINDS):

time: 24.1 us -> 24.3 us (level)
  no operation moved by 1% of the time
where the time goes in v11:
time: 24.3 us; the launch traced here: 23.9 us
  Pallas kernels  23.3 us (96%)
  local copies, waits for them, and re-layouts  0.6 us (2%)
    pallas_call x1, Pallas kernels, per_device(): pl.pallas_call(kernel, out_shape=pltpu.VMEM((1, COLS), jnp.bfloat16), in_...  23.3 us
    unnamed x1, local copies, waits for them, and re-layouts  0.6 us

profile of v11, /device:TPU:1, one launch (start us, length us, event | category | flops | bytes accessed | tf_op | source)
XLA Modules:
  0.0 23.9 jit_solution(346258012242668630)
XLA Ops:
  0.0 23.3 %decode.1 = bf16[1,1280]{1,0:T(2,128)(2,1)S(1)} custom-call(bf16[1,2,8,128]{3,2,1,0:T(8,128)(2,1)} %q_hbm.1, bf16[32,2,512,128]{3,2,1,0:T(8,128)(2,1)} %k_hbm.1, bf16[32,2,512,128]{3,2,1,0:T(8,128)(2,1)} %v_hbm.1, s32[32]{0:T(128)} %len_hbm.1, bf16[2,8,128,5120]{3,2,1,0:T(8,128)(2,1)} %w_hbm.1), custom_call_target="tpu_custom_call" | custom-call | tf_op jit(solution)/shard_map/decode/pallas_call | solution.py:316
  23.3 0.6 %copy.7 = bf16[1,1280]{1,0:T(2,128)(2,1)} copy(bf16[1,1280]{1,0:T(2,128)(2,1)S(1)} %decode.1) | data formatting | bytes 5120

commit v12 on v9

--- a/solution.py
+++ b/solution.py
@@ -195,14 +195,15 @@
     def _(i):
         n = 2 * i + 1
         now, second, third = nth(n), nth(n + 1), nth(n + 2)
-        for step in (second, third):
-            arrived(2 * step)
-            arrived(2 * step + 1)
+        arrived(2 * second)
+        arrived(2 * second + 1)
         loaded(n + 1)
-        loaded(n + 2)
         scores(second, 0)
         reads(now, 1)
         send(now)
+        arrived(2 * third)
+        arrived(2 * third + 1)
+        loaded(n + 2)
         scores(third, 1)
         reads(second, 0)
         send(second)

time: 24.1 us -> 24.1 us (level)
  no operation moved by 1% of the time
where the time goes in v12:
time: 24.1 us; the launch traced here: 24 us
  Pallas kernels  23.4 us (97%)
  local copies, waits for them, and re-layouts  0.6 us (2%)
    pallas_call x1, Pallas kernels, per_device(): pl.pallas_call(kernel, out_shape=pltpu.VMEM((1, COLS), jnp.bfloat16), in_...  23.4 us
    unnamed x1, local copies, waits for them, and re-layouts  0.6 us

profile of v12, /device:TPU:1, one launch (start us, length us, event | category | flops | bytes accessed | tf_op | source)
XLA Modules:
  0.0 24.0 jit_solution(11599409859072496606)
XLA Ops:
  0.0 23.4 %decode.1 = bf16[1,1280]{1,0:T(2,128)(2,1)S(1)} custom-call(bf16[1,2,8,128]{3,2,1,0:T(8,128)(2,1)} %q_hbm.1, bf16[32,2,512,128]{3,2,1,0:T(8,128)(2,1)} %k_hbm.1, bf16[32,2,512,128]{3,2,1,0:T(8,128)(2,1)} %v_hbm.1, s32[32]{0:T(128)} %len_hbm.1, bf16[2,8,128,5120]{3,2,1,0:T(8,128)(2,1)} %w_hbm.1), custom_call_target="tpu_custom_call" | custom-call | tf_op jit(solution)/shard_map/decode/pallas_call | solution.py:306
  23.4 0.6 %copy.7 = bf16[1,1280]{1,0:T(2,128)(2,1)} copy(bf16[1,1280]{1,0:T(2,128)(2,1)S(1)} %decode.1) | data formatting | bytes 5120

commit v13 on v9

--- a/solution.py
+++ b/solution.py
@@ -208,8 +208,9 @@
         send(second)
 
     pltpu.make_async_copy(wbuf, wbuf, w_sem.at[0]).wait()
-    reads(nth(STEPS - 1), 1)
-    send(nth(STEPS - 1))
+    for units in (head, tail):
+        reads(nth(STEPS - 1), 1, units)
+        send(nth(STEPS - 1), units)
     parts[me] = psend[me]
     stats[pl.ds(me, 1)] = ssend[pl.ds(me, 1)]
 

time: 24.1 us -> 24.2 us (level)
  no operation moved by 1% of the time
where the time goes in v13:
time: 24.2 us; the launch traced here: 24 us
  Pallas kernels  23.4 us (97%)
  local copies, waits for them, and re-layouts  0.6 us (2%)
    pallas_call x1, Pallas kernels, per_device(): pl.pallas_call(kernel, out_shape=pltpu.VMEM((1, COLS), jnp.bfloat16), in_...  23.4 us
    unnamed x1, local copies, waits for them, and re-layouts  0.6 us

profile of v13, /device:TPU:1, one launch (start us, length us, event | category | flops | bytes accessed | tf_op | source)
XLA Modules:
  0.0 24.0 jit_solution(17179153298627165856)
XLA Ops:
  0.0 23.4 %decode.1 = bf16[1,1280]{1,0:T(2,128)(2,1)S(1)} custom-call(bf16[1,2,8,128]{3,2,1,0:T(8,128)(2,1)} %q_hbm.1, bf16[32,2,512,128]{3,2,1,0:T(8,128)(2,1)} %k_hbm.1, bf16[32,2,512,128]{3,2,1,0:T(8,128)(2,1)} %v_hbm.1, s32[32]{0:T(128)} %len_hbm.1, bf16[2,8,128,5120]{3,2,1,0:T(8,128)(2,1)} %w_hbm.1), custom_call_target="tpu_custom_call" | custom-call | tf_op jit(solution)/shard_map/decode/pallas_call | solution.py:306
  23.4 0.6 %copy.7 = bf16[1,1280]{1,0:T(2,128)(2,1)} copy(bf16[1,1280]{1,0:T(2,128)(2,1)S(1)} %decode.1) | data formatting | bytes 5120

commit v14 on v9

--- a/solution.py
+++ b/solution.py
@@ -173,8 +173,8 @@
 
             @pl.when(b != me)
             def _():
+                p_remote(b).start()
                 s_remote(b).start()
-                p_remote(b).start()
 
     head, tail = range(PAIR), range(PAIR, UNIT)
     arrived(0)

time: 24.1 us -> 24.6 us (1.021)
  the two profiles are of different devices: /device:TPU:1 before, /device:TPU:39 now
where the time goes in v14:
time: 24.6 us; the launch traced here: 24.5 us
  Pallas kernels  23.9 us (97%)
  local copies, waits for them, and re-layouts  0.6 us (2%)
    pallas_call x1, Pallas kernels, per_device(): pl.pallas_call(kernel, out_shape=pltpu.VMEM((1, COLS), jnp.bfloat16), in_...  23.9 us
    unnamed x1, local copies, waits for them, and re-layouts  0.6 us

profile of v14, /device:TPU:39, one launch (start us, length us, event | category | flops | bytes accessed | tf_op | source)
XLA Modules:
  0.0 24.5 jit_solution(13321639021816311694)
XLA Ops:
  0.0 23.9 %decode.1 = bf16[1,1280]{1,0:T(2,128)(2,1)S(1)} custom-call(bf16[1,2,8,128]{3,2,1,0:T(8,128)(2,1)} %q_hbm.1, bf16[32,2,512,128]{3,2,1,0:T(8,128)(2,1)} %k_hbm.1, bf16[32,2,512,128]{3,2,1,0:T(8,128)(2,1)} %v_hbm.1, s32[32]{0:T(128)} %len_hbm.1, bf16[2,8,128,5120]{3,2,1,0:T(8,128)(2,1)} %w_hbm.1), custom_call_target="tpu_custom_call" | custom-call | tf_op jit(solution)/shard_map/decode/pallas_call | solution.py:305
  23.9 0.6 %copy.7 = bf16[1,1280]{1,0:T(2,128)(2,1)} copy(bf16[1,1280]{1,0:T(2,128)(2,1)S(1)} %decode.1) | data formatting | bytes 5120

commit v15 on v9

--- a/solution.py
+++ b/solution.py
@@ -92,7 +92,7 @@
     q_copy.wait()
     len_copy.wait()
     pl.semaphore_wait(barrier, SEQ - 1 + PAIR * (GRP - 1))
-    for z in (3, 2, 1, 0):
+    for z in (3, 1, 2, 0):
         for x in (2, 3, 1, 0):
             for peer in range(z * ROW + x * PAIR, z * ROW + x * PAIR + PAIR):
 

time: 24.1 us -> 24.2 us (level)
  no operation moved by 1% of the time
where the time goes in v15:
time: 24.2 us; the launch traced here: 24.1 us
  Pallas kernels  23.5 us (97%)
  local copies, waits for them, and re-layouts  0.6 us (2%)
    pallas_call x1, Pallas kernels, per_device(): pl.pallas_call(kernel, out_shape=pltpu.VMEM((1, COLS), jnp.bfloat16), in_...  23.5 us
    unnamed x1, local copies, waits for them, and re-layouts  0.6 us

profile of v15, /device:TPU:1, one launch (start us, length us, event | category | flops | bytes accessed | tf_op | source)
XLA Modules:
  0.0 24.1 jit_solution(2702076895672194030)
XLA Ops:
  0.0 23.5 %decode.1 = bf16[1,1280]{1,0:T(2,128)(2,1)S(1)} custom-call(bf16[1,2,8,128]{3,2,1,0:T(8,128)(2,1)} %q_hbm.1, bf16[32,2,512,128]{3,2,1,0:T(8,128)(2,1)} %k_hbm.1, bf16[32,2,512,128]{3,2,1,0:T(8,128)(2,1)} %v_hbm.1, s32[32]{0:T(128)} %len_hbm.1, bf16[2,8,128,5120]{3,2,1,0:T(8,128)(2,1)} %w_hbm.1), custom_call_target="tpu_custom_call" | custom-call | tf_op jit(solution)/shard_map/decode/pallas_call | solution.py:305
  23.5 0.6 %copy.7 = bf16[1,1280]{1,0:T(2,128)(2,1)} copy(bf16[1,1280]{1,0:T(2,128)(2,1)S(1)} %decode.1) | data formatting | bytes 5120
